TPU v7x, 32 devices: a whole 2x2x4 slice. The times are simulated.
32 devices in a mesh: dp: 16 (over z, x, core), tp: 2 (over y).
Axes of the slice: x: 2, y: 2, z: 4, core: 2. Of those that a mesh axis runs over, the one named last changes fastest.
Arguments:
- tokens: bfloat16 [4096, 2048], P(('dp', 'tp')), may hold values from -6 to 6
- gain_attn: bfloat16 [2048], P('dp'), may hold values from 0.5 to 1.5
- query_weight: bfloat16 [2048, 2048], P('dp', 'tp'), may hold values from -0.125 to 0.125
- key_matrix: bfloat16 [2048, 512], P('dp', 'tp'), may hold values from -0.125 to 0.125
- value_matrix: bfloat16 [2048, 512], P('dp', 'tp'), may hold values from -0.125 to 0.125
- out_weight: bfloat16 [2048, 2048], P('tp', 'dp'), may hold values from -1 to 1
- gain_ffn: bfloat16 [2048], P('dp'), may hold values from 0.5 to 1.5
- gate_weight: bfloat16 [2048, 8192], P('dp', 'tp'), may hold values from -0.125 to 0.125
- up_weight: bfloat16 [2048, 8192], P('dp', 'tp'), may hold values from -0.125 to 0.125
- down_weight: bfloat16 [8192, 2048], P('tp', 'dp'), may hold values from -0.0625 to 0.0625
- cotangent: bfloat16 [4096, 2048], P(('dp', 'tp')), may hold values from -6 to 6
- seq_lens: int32 [16], P('dp'), may hold values from 128 to 256, as said below
- pad_mask: int32 [4096], P('dp'), may hold values from 0 to 1, as said below
- positions: int32 [4096], P('dp'), may hold values from 0 to 255, as said below
Outputs:
- output: bfloat16 [4096, 2048], P(('dp', 'tp'))
- grad_tokens: float32 [4096, 2048], P(('dp', 'tp'))
- grad_gain_attn: float32 [2048], P(('dp', 'tp'))
- grad_query: float32 [2048, 2048], P('dp', 'tp')
- grad_key: float32 [2048, 512], P('dp', 'tp')
- grad_value: float32 [2048, 512], P('dp', 'tp')
- grad_out: float32 [2048, 2048], P('tp', 'dp')
- grad_gain_ffn: float32 [2048], P(('dp', 'tp'))
- grad_gate: float32 [2048, 8192], P('dp', 'tp')
- grad_up: float32 [2048, 8192], P('dp', 'tp')
- grad_down: float32 [8192, 2048], P('tp', 'dp')
Inputs may be any that keep to these rules, and one draw needn't show every extreme that they name: Bucket b holds one sequence in its first seq_lens[b] slots; the slots after it are padding. `pad_mask`: every slot after a bucket's sequence is padding; the whole first bucket is live. `positions`: inside a bucket's sequence a token's position counts the live tokens before it; the padding after the sequence has position 0.
All inputs are finite; a program needn't handle non-finite values.
Results may differ from a plain program's by a relative error of at most 0.013.
Values may be sent and summed in bfloat16 or wider, within the bound.
No kernel may reach another device: no remote copies, remote signals or barrier semaphores. Data moves between devices by JAX's collectives and lax.ppermute only.
A program may use at most 256 MiB of HBM per device.

v0:
```python
import math

import jax
import jax.numpy as jnp
import numpy as np
from jax import lax
from jax.sharding import PartitionSpec as P

HEAD_SIZE = 64


eps = 1e-05
rope_theta = 500000.0


def rope_table(head_dim):
    half_dim = head_dim // 2
    base_freq = 1.0 / rope_theta ** (np.arange(half_dim) * 2.0 / head_dim)
    wavelen = 2.0 * math.pi / base_freq
    smooth = (8192.0 / wavelen - 1.0) / 3.0
    middle = (1.0 - smooth) * base_freq / 32.0 + smooth * base_freq
    return np.where(
        wavelen > 8192.0, base_freq / 32.0, np.where(wavelen < 2048.0, base_freq, middle)
    )


def root_norm(inputs, gain_vec):
    inverse_rms = lax.rsqrt(jnp.mean(inputs * inputs, axis=1, keepdims=True) + eps)
    return inputs * inverse_rms * gain_vec[None, :]


def rotary_apply(heads, cosine_lookup, sine_lookup, turn):
    half_dim = heads.shape[-1] // 2
    cosine_part = cosine_lookup[:, None, :]
    sine_part = turn * sine_lookup[:, None, :]
    front_half = heads[..., :half_dim]
    back_half = heads[..., half_dim:]
    return jnp.concatenate(
        [
            front_half * cosine_part - back_half * sine_part,
            back_half * cosine_part + front_half * sine_part,
        ],
        axis=-1,
    )


def allowed_mask(seq_length, live_mask, slot_count):
    slot_ids = jnp.arange(slot_count, dtype=jnp.int32)
    segment = (slot_ids >= seq_length).astype(jnp.int32)
    same_seq = segment[:, None] == segment[None, :]
    causal = slot_ids[None, :] <= slot_ids[:, None]
    keyed = (live_mask[None, :] == 1) | (slot_ids[:, None] == slot_ids[None, :])
    return same_seq & causal & keyed


def contract_rows(left, right):
    return lax.dot_general(
        left, right, (((0,), (0,)), ((), ())), preferred_element_type=jnp.float32
    )


def contract_cols(left, right):
    return lax.dot_general(
        left, right, (((1,), (1,)), ((), ())), preferred_element_type=jnp.float32
    )


def shards(
    tokens,
    gain_attn,
    query_weight,
    key_matrix,
    value_matrix,
    out_weight,
    gain_ffn,
    gate_weight,
    up_weight,
    down_weight,
    cotangent,
    seq_lens,
    pad_mask,
    positions,
):
    group_rows = pad_mask.shape[0]
    heads_kv = key_matrix.shape[1] // HEAD_SIZE
    heads_query = query_weight.shape[1] // HEAD_SIZE
    group_size = heads_query // heads_kv
    score_scale = 1.0 / math.sqrt(HEAD_SIZE)
    attention_set = (
        lax.all_gather(gain_attn, "dp", axis=0, tiled=True),
        lax.all_gather(query_weight, "dp", axis=0, tiled=True),
        lax.all_gather(key_matrix, "dp", axis=0, tiled=True),
        lax.all_gather(value_matrix, "dp", axis=0, tiled=True),
        lax.all_gather(out_weight, "dp", axis=1, tiled=True),
    )
    gain_one, query_full, key_full, value_full, out_full = attention_set
    inputs_wide = tokens.astype(jnp.float32)
    normed_one = root_norm(inputs_wide, gain_one.astype(jnp.float32)).astype(jnp.bfloat16)
    piece = lax.all_gather(normed_one, "tp", axis=0, tiled=True)
    normed_one_all = piece
    query_raw = jnp.dot(piece, query_full, preferred_element_type=jnp.float32)
    key_raw = jnp.dot(piece, key_full, preferred_element_type=jnp.float32)
    value_raw = jnp.dot(piece, value_full, preferred_element_type=jnp.float32)
    inverse_freq = jnp.asarray(rope_table(HEAD_SIZE), jnp.float32)
    angles = positions.astype(jnp.float32)[:, None] * inverse_freq[None, :]
    cosine_lookup = jnp.cos(angles)
    sine_lookup = jnp.sin(angles)
    query_head_split = rotary_apply(
        query_raw.reshape(group_rows, heads_query, HEAD_SIZE), cosine_lookup, sine_lookup, 1.0
    )
    query_head_split = query_head_split.astype(jnp.bfloat16).reshape(
        group_rows, heads_kv, group_size, HEAD_SIZE
    )
    key_head_split = rotary_apply(
        key_raw.reshape(group_rows, heads_kv, HEAD_SIZE), cosine_lookup, sine_lookup, 1.0
    ).astype(jnp.bfloat16)
    value_head_split = value_raw.astype(jnp.bfloat16).reshape(group_rows, heads_kv, HEAD_SIZE)
    allowed = allowed_mask(seq_lens[0], pad_mask, group_rows)
    scores = (
        jnp.einsum(
            "qgmd,kgd->gmqk", query_head_split, key_head_split, preferred_element_type=jnp.float32
        )
        * score_scale
    )
    scores = jnp.where(allowed[None, None], scores, -1e30)
    row_peak = jnp.max(scores, axis=-1, keepdims=True)
    log_total = row_peak + jnp.log(jnp.sum(jnp.exp(scores - row_peak), axis=-1, keepdims=True))
    probs_low = jnp.exp(scores - log_total).astype(jnp.bfloat16)
    attended = jnp.einsum(
        "gmqk,kgd->qgmd", probs_low, value_head_split, preferred_element_type=jnp.float32
    )
    attended = attended.reshape(group_rows, heads_query * HEAD_SIZE).astype(jnp.bfloat16)
    rows_taken = attended
    branch_attn = lax.psum_scatter(
        jnp.dot(rows_taken, out_full, preferred_element_type=jnp.float32),
        "tp",
        scatter_dimension=0,
        tiled=True,
    )
    resid = inputs_wide + branch_attn
    feed_set = (
        lax.all_gather(gain_ffn, "dp", axis=0, tiled=True),
        lax.all_gather(gate_weight, "dp", axis=0, tiled=True),
        lax.all_gather(up_weight, "dp", axis=0, tiled=True),
        lax.all_gather(down_weight, "dp", axis=1, tiled=True),
    )
    gain_two, gate_full, up_full, down_full = feed_set
    normed_two = root_norm(resid, gain_two.astype(jnp.float32)).astype(jnp.bfloat16)
    piece = lax.all_gather(normed_two, "tp", axis=0, tiled=True)
    normed_two_all = piece
    gate_proj = jnp.dot(piece, gate_full, preferred_element_type=jnp.float32)
    up_proj = jnp.dot(piece, up_full, preferred_element_type=jnp.float32)
    hidden = (jax.nn.silu(gate_proj) * up_proj).astype(jnp.bfloat16)
    rows_taken = hidden
    branch_feed = lax.psum_scatter(
        jnp.dot(rows_taken, down_full, preferred_element_type=jnp.float32).astype(jnp.bfloat16),
        "tp",
        scatter_dimension=0,
        tiled=True,
    ).astype(jnp.float32)
    output = (resid + branch_feed).astype(jnp.bfloat16)
    feed_back = (
        lax.all_gather(gain_ffn, "dp", axis=0, tiled=True),
        lax.all_gather(gate_weight, "dp", axis=0, tiled=True),
        lax.all_gather(up_weight, "dp", axis=0, tiled=True),
        lax.all_gather(down_weight, "dp", axis=1, tiled=True),
    )
    gain_two_back, gate_back, up_back, down_back = feed_back
    piece = lax.all_gather(cotangent, "tp", axis=0, tiled=True)
    cotangent_all = piece
    hidden_grad = contract_cols(piece, down_back)
    sigmoid_gate = jax.nn.sigmoid(gate_proj)
    gate_active = gate_proj * sigmoid_gate
    gate_grad = (
        hidden_grad * up_proj * sigmoid_gate * (1.0 + gate_proj * (1.0 - sigmoid_gate))
    ).astype(jnp.bfloat16)
    up_grad = (hidden_grad * gate_active).astype(jnp.bfloat16)
    grad_down = contract_rows(hidden, cotangent_all)
    grad_gate = contract_rows(normed_two_all, gate_grad)
    grad_up = contract_rows(normed_two_all, up_grad)
    normed_two_grad = lax.psum_scatter(
        contract_cols(gate_grad, gate_back) + contract_cols(up_grad, up_back),
        "tp",
        scatter_dimension=0,
        tiled=True,
    )
    norm_pull = jax.vjp(root_norm, resid, gain_two_back.astype(jnp.float32))[1]
    resid_part, gain_two_grad = norm_pull(normed_two_grad)
    resid_grad = cotangent.astype(jnp.float32) + resid_part
    attention_back = (
        lax.all_gather(gain_attn, "dp", axis=0, tiled=True),
        lax.all_gather(query_weight, "dp", axis=0, tiled=True),
        lax.all_gather(key_matrix, "dp", axis=0, tiled=True),
        lax.all_gather(value_matrix, "dp", axis=0, tiled=True),
        lax.all_gather(out_weight, "dp", axis=1, tiled=True),
    )
    gain_one_back, query_back, key_back, value_back, out_back = attention_back
    resid_low = resid_grad.astype(jnp.bfloat16)
    piece = lax.all_gather(resid_low, "tp", axis=0, tiled=True)
    attended_grad = contract_cols(piece, out_back)
    grad_out = contract_rows(attended, piece)
    attended_heads = attended_grad.astype(jnp.bfloat16).reshape(
        group_rows, heads_kv, group_size, HEAD_SIZE
    )
    probs_full = jnp.exp(scores - log_total)
    prob_grad = jnp.einsum(
        "qgmd,kgd->gmqk", attended_heads, value_head_split, preferred_element_type=jnp.float32
    )
    row_delta = jnp.sum(prob_grad * probs_full, axis=-1, keepdims=True)
    score_grad = (probs_full * (prob_grad - row_delta)).astype(jnp.bfloat16)
    value_grad = jnp.einsum(
        "gmqk,qgmd->kgd", probs_low, attended_heads, preferred_element_type=jnp.float32
    )
    value_grad = value_grad.reshape(group_rows, heads_kv * HEAD_SIZE).astype(jnp.bfloat16)
    query_grad = (
        jnp.einsum("gmqk,kgd->qgmd", score_grad, key_head_split, preferred_element_type=jnp.float32)
        * score_scale
    )
    query_grad = rotary_apply(
        query_grad.reshape(group_rows, heads_query, HEAD_SIZE), cosine_lookup, sine_lookup, -1.0
    )
    query_grad = query_grad.reshape(group_rows, heads_query * HEAD_SIZE).astype(jnp.bfloat16)
    key_grad = (
        jnp.einsum(
            "gmqk,qgmd->kgd", score_grad, query_head_split, preferred_element_type=jnp.float32
        )
        * score_scale
    )
    key_grad = (
        rotary_apply(key_grad, cosine_lookup, sine_lookup, -1.0)
        .reshape(group_rows, heads_kv * HEAD_SIZE)
        .astype(jnp.bfloat16)
    )
    grad_query = contract_rows(normed_one_all, query_grad)
    grad_key = contract_rows(normed_one_all, key_grad)
    grad_value = contract_rows(normed_one_all, value_grad)
    normed_one_grad = lax.psum_scatter(
        contract_cols(query_grad, query_back)
        + contract_cols(key_grad, key_back)
        + contract_cols(value_grad, value_back),
        "tp",
        scatter_dimension=0,
        tiled=True,
    )
    norm_pull_one = jax.vjp(root_norm, inputs_wide, gain_one_back.astype(jnp.float32))[1]
    token_part, gain_one_grad = norm_pull_one(normed_one_grad)
    token_grad = resid_grad + token_part
    weight_grads = (
        lax.psum_scatter(grad_query, "dp", scatter_dimension=0, tiled=True),
        lax.psum_scatter(grad_key, "dp", scatter_dimension=0, tiled=True),
        lax.psum_scatter(grad_value, "dp", scatter_dimension=0, tiled=True),
        lax.psum_scatter(grad_out, "dp", scatter_dimension=1, tiled=True),
        lax.psum_scatter(grad_gate, "dp", scatter_dimension=0, tiled=True),
        lax.psum_scatter(grad_up, "dp", scatter_dimension=0, tiled=True),
        lax.psum_scatter(grad_down, "dp", scatter_dimension=1, tiled=True),
    )
    gain_grads = (
        lax.psum_scatter(gain_one_grad, ("dp", "tp"), scatter_dimension=0, tiled=True),
        lax.psum_scatter(gain_two_grad, ("dp", "tp"), scatter_dimension=0, tiled=True),
    )
    return (
        output,
        token_grad,
        gain_grads[0],
        weight_grads[0],
        weight_grads[1],
        weight_grads[2],
        weight_grads[3],
        gain_grads[1],
        weight_grads[4],
        weight_grads[5],
        weight_grads[6],
    )


def solution(mesh):
    placed = (
        P(("dp", "tp"), None),
        P("dp"),
        P("dp", "tp"),
        P("dp", "tp"),
        P("dp", "tp"),
        P("tp", "dp"),
        P("dp"),
        P("dp", "tp"),
        P("dp", "tp"),
        P("tp", "dp"),
        P(("dp", "tp"), None),
        P("dp"),
        P("dp"),
        P("dp"),
    )
    return jax.shard_map(
        shards,
        mesh=mesh,
        in_specs=placed,
        out_specs=(
            P(("dp", "tp"), None),
            P(("dp", "tp"), None),
            P(("dp", "tp")),
            P("dp", "tp"),
            P("dp", "tp"),
            P("dp", "tp"),
            P("tp", "dp"),
            P(("dp", "tp")),
            P("dp", "tp"),
            P("dp", "tp"),
            P("tp", "dp"),
        ),
        check_vma=False,
    )
```

profile of v0, /device:TPU:0, one launch (start us, length us, event | category | flops | bytes accessed | tf_op | source)
XLA Modules:
  0.0 2231.0 jit_solution(2233070390989913457)
XLA Ops:
  7.2 23.3 %all-gather = bf16[16,1,128]{2,1,0:T(2,128)(2,1)S(1)} all-gather(bf16[1,1,128]{2,1,0:T(2,128)(2,1)} %bitcast.155), channel_id=1, replica_groups=mesh['dp'=16,'tp'=2] {'dp'}, dimensions={0}, use_global_device_ids=true | all-gather | bytes 4352 | tf_op jit(solution)/shard_map/all_gather | solution.py:90
  39.6 13.0 all-gather.14.cloned.1.call-done
  52.6 40.0 %all-gather.18.cloned.1.call-done = bf16[2048,256]{1,0:T(8,128)(2,1)} async-done(((bf16[128,256]{1,0:T(8,128)(2,1)}), bf16[2048,256]{1,0:T(8,128)(2,1)}) %all-gather.18.cloned.1.call-update) | async-done | bytes 1048592 | tf_op jit(solution)/shard_map/all_gather | solution.py:92
  94.7 36.9 %all-gather.16.cloned.1.call-done = bf16[2048,256]{1,0:T(8,128)(2,1)} async-done(((bf16[128,256]{1,0:T(8,128)(2,1)}), bf16[2048,256]{1,0:T(8,128)(2,1)}) %all-gather.16.cloned.1.call-update) | async-done | bytes 1048592 | tf_op jit(solution)/shard_map/all_gather | solution.py:93
  133.7 49.3 %all-gather.20.cloned.1.call-done = bf16[2048,1024]{1,0:T(8,128)(2,1)} async-done(((bf16[128,1024]{1,0:T(8,128)(2,1)}), bf16[2048,1024]{1,0:T(8,128)(2,1)}) %all-gather.20.cloned.1.call-update) | async-done | bytes 4194320 | tf_op jit(solution)/shard_map/all_gather | solution.py:91
  191.7 44.4 %all-gather.22.cloned.1.call-done = bf16[1024,2048]{1,0:T(8,128)(2,1)} async-done(((bf16[1024,128]{1,0:T(8,128)(2,1)}), bf16[1024,2048]{1,0:T(8,128)(2,1)}) %all-gather.22.cloned.1.call-update) | async-done | bytes 4194320 | tf_op jit(solution)/shard_map/all_gather | solution.py:94
  241.0 18.5 all-gather.1
  277.4 18.1 all-gather.24.cloned.1.call-done
  295.5 128.6 %all-gather.26.cloned.1.call-done = bf16[2048,4096]{1,0:T(8,128)(2,1)} async-done(((bf16[128,4096]{1,0:T(8,128)(2,1)}), bf16[2048,4096]{1,0:T(8,128)(2,1)}) %all-gather.26.cloned.1.call-update) | async-done | bytes 16777232 | tf_op jit(solution)/shard_map/all_gather | solution.py:143
  436.7 114.2 %all-gather.28.cloned.1.call-done = bf16[2048,4096]{1,0:T(8,128)(2,1)} async-done(((bf16[128,4096]{1,0:T(8,128)(2,1)}), bf16[2048,4096]{1,0:T(8,128)(2,1)}) %all-gather.28.cloned.1.call-update) | async-done | bytes 16777232 | tf_op jit(solution)/shard_map/all_gather | solution.py:144
  571.8 132.1 %all-gather.30.cloned.1.call-done = bf16[4096,2048]{1,0:T(8,128)(2,1)} async-done(((bf16[4096,128]{1,0:T(8,128)(2,1)}), bf16[4096,2048]{1,0:T(8,128)(2,1)}) %all-gather.30.cloned.1.call-update) | async-done | bytes 16777232 | tf_op jit(solution)/shard_map/all_gather | solution.py:145
  703.9 13.5 multiply_convert_fusion
  742.6 30.2 %reduce-scatter.16.cloned.1.call-done = f32[128,2048]{1,0:T(8,128)} async-done(((f32[256,2048]{1,0:T(8,128)}), f32[128,2048]{1,0:T(8,128)}) %reduce-scatter.16.cloned.1.call-update) | async-done | bytes 1048592 | tf_op jit(solution)/shard_map/reduce_scatter | solution.py:181
  778.3 21.2 all-gather.34.cloned.1.call-done
  848.0 15.1 fusion.44
  863.2 14.8 fusion.45
  879.2 15.5 fusion.46
  897.5 39.8 %all-reduce.2 = (f32[2048]{0:T(1024)S(1)}, f32[2048]{0:T(1024)S(1)}) all-reduce(f32[2048]{0:T(1024)S(1)} %get-tuple-element.13, f32[2048]{0:T(1024)S(1)} %get-tuple-element.11), channel_id=6, replica_groups=mesh['dp'=16,'tp'=2] {'dp','tp'}, use_global_device_ids=true, to_apply=%region_12.13.clone | all-reduce | flops 4096 | bytes 32768
  941.5 63.8 %reduce-scatter.24.cloned.1.call-done = f32[128,256]{1,0:T(8,128)} async-done(((f32[2048,256]{1,0:T(8,128)}), f32[128,256]{1,0:T(8,128)}) %reduce-scatter.24.cloned.1.call-update) | async-done | bytes 131088 | tf_op jit(solution)/shard_map/reduce_scatter | solution.py:251
  1005.3 106.9 %reduce-scatter.20.cloned.1.call-done = f32[128,1024]{1,0:T(8,128)} async-done(((f32[2048,1024]{1,0:T(8,128)}), f32[128,1024]{1,0:T(8,128)}) %reduce-scatter.20.cloned.1.call-update) | async-done | bytes 524304 | tf_op jit(solution)/shard_map/reduce_scatter | solution.py:249
  1112.2 107.9 %reduce-scatter.26.cloned.1.call-done = f32[1024,128]{1,0:T(8,128)} async-done(((f32[1024,2048]{1,0:T(8,128)}), f32[1024,128]{1,0:T(8,128)}) %reduce-scatter.26.cloned.1.call-update) | async-done | bytes 524304 | tf_op jit(solution)/shard_map/reduce_scatter | solution.py:252
  1220.1 334.9 %reduce-scatter.28.cloned.1.call-done = f32[128,4096]{1,0:T(8,128)} async-done(((f32[2048,4096]{1,0:T(8,128)}), f32[128,4096]{1,0:T(8,128)}) %reduce-scatter.28.cloned.1.call-update) | async-done | bytes 2097168 | tf_op jit(solution)/shard_map/reduce_scatter | solution.py:253
  1555.0 334.5 %reduce-scatter.30.cloned.1.call-done = f32[128,4096]{1,0:T(8,128)} async-done(((f32[2048,4096]{1,0:T(8,128)}), f32[128,4096]{1,0:T(8,128)}) %reduce-scatter.30.cloned.1.call-update) | async-done | bytes 2097168 | tf_op jit(solution)/shard_map/reduce_scatter | solution.py:254
  1889.4 334.3 %reduce-scatter.32.cloned.1.call-done = f32[4096,128]{1,0:T(8,128)} async-done(((f32[4096,2048]{1,0:T(8,128)}), f32[4096,128]{1,0:T(8,128)}) %reduce-scatter.32.cloned.1.call-update) | async-done | bytes 2097168 | tf_op jit(solution)/shard_map/reduce_scatter | solution.py:255
  (176 shorter events, 164.3 us)
Async XLA Ops:
  7.2 45.4 %all-gather.14.cloned.1.call-start = ((), (), s32[]{:S(2)}) async-start(), calls=%async_computation.11 | async-start | bytes 1572864 | tf_op jit(solution)/shard_map/all_gather | solution.py:99
  33.8 58.7 %all-gather.18.cloned.1.call-start = ((), (), s32[]{:S(2)}) async-start(), calls=%async_computation.13 | async-start | bytes 1114112 | tf_op jit(solution)/shard_map/all_gather | solution.py:92
  34.6 97.0 %all-gather.16.cloned.1.call-start = ((), (), s32[]{:S(2)}) async-start(), calls=%async_computation.12 | async-start | bytes 1114112 | tf_op jit(solution)/shard_map/all_gather | solution.py:93
  35.3 147.7 %all-gather.20.cloned.1.call-start = ((), (), s32[]{:S(2)}) async-start(), calls=%async_computation.14 | async-start | bytes 4456448 | tf_op jit(solution)/shard_map/all_gather | solution.py:91
  35.9 200.2 %all-gather.22.cloned.1.call-start = ((), (), s32[]{:S(2)}) async-start(), calls=%async_computation.15 | async-start | bytes 4456448 | tf_op jit(solution)/shard_map/all_gather | solution.py:94
  36.5 234.7 %reduce-scatter.12.cloned.1.call-start = ((), (), s32[]{:S(2)}) async-start(), calls=%async_computation.16 | async-start | bytes 3145728 | tf_op jit(solution)/shard_map/reduce_scatter | solution.py:134
  52.6 130.4 %copy-start.2 = (bf16[256,2048]{1,0:T(8,128)(2,1)S(1)}, bf16[256,2048]{1,0:T(8,128)(2,1)}, u32[]{:S(2)}) copy-start(bf16[256,2048]{1,0:T(8,128)(2,1)} %all-gather.14.cloned.1.call-done) | copy-start | bytes 3145732
  240.9 54.6 %all-gather.24.cloned.1.call-start = ((), (), s32[]{:S(2)}) async-start(), calls=%async_computation.17 | async-start | bytes 1572864 | tf_op jit(solution)/shard_map/all_gather | solution.py:149
  274.1 150.0 %all-gather.26.cloned.1.call-start = ((), (), s32[]{:S(2)}) async-start(), calls=%async_computation.18 | async-start | bytes 17825792 | tf_op jit(solution)/shard_map/all_gather | solution.py:143
  274.9 276.1 %all-gather.28.cloned.1.call-start = ((), (), s32[]{:S(2)}) async-start(), calls=%async_computation.19 | async-start | bytes 17825792 | tf_op jit(solution)/shard_map/all_gather | solution.py:144
  275.6 296.2 %all-gather.32.cloned.1.call-start = ((), (), s32[]{:S(2)}) async-start(), calls=%async_computation.22 | async-start | bytes 1572864 | tf_op jit(solution)/shard_map/all_gather | solution.py:169
  276.2 427.7 %all-gather.30.cloned.1.call-start = ((), (), s32[]{:S(2)}) async-start(), calls=%async_computation.20 | async-start | bytes 17825792 | tf_op jit(solution)/shard_map/all_gather | solution.py:145
  276.9 495.9 %reduce-scatter.16.cloned.1.call-start = ((), (), s32[]{:S(2)}) async-start(), calls=%async_computation.23 | async-start | bytes 3145728 | tf_op jit(solution)/shard_map/reduce_scatter | solution.py:181
  295.5 255.4 %copy-start.6 = (bf16[256,2048]{1,0:T(8,128)(2,1)S(1)}, bf16[256,2048]{1,0:T(8,128)(2,1)}, u32[]{:S(2)}) copy-start(bf16[256,2048]{1,0:T(8,128)(2,1)} %all-gather.24.cloned.1.call-done) | copy-start | bytes 3145732
  742.5 56.9 %all-gather.34.cloned.1.call-start = ((), (), s32[]{:S(2)}) async-start(), calls=%async_computation.24 | async-start | bytes 1572864 | tf_op jit(solution)/shard_map/all_gather | solution.py:199
  778.0 116.8 %reduce-scatter.18.cloned.1.call-start = ((), (), s32[]{:S(2)}) async-start(), calls=%async_computation.25 | async-start | bytes 3145728 | tf_op jit(solution)/shard_map/reduce_scatter | solution.py:237
  819.1 119.3 %reduce-scatter.14.cloned.1.call-start = ((), (), s32[]{:S(2)}) async-start(), calls=%async_computation.21 | async-start | bytes 1572864 | tf_op jit(solution)/shard_map/reduce_scatter | solution.py:155
  831.4 110.1 %reduce-scatter.22.cloned.1.call-start = ((), (), s32[]{:S(2)}) async-start(), calls=%async_computation.27 | async-start | bytes 2228224 | tf_op jit(solution)/shard_map/reduce_scatter | solution.py:250
  833.3 172.0 %reduce-scatter.24.cloned.1.call-start = ((), (), s32[]{:S(2)}) async-start(), calls=%async_computation.28 | async-start | bytes 2228224 | tf_op jit(solution)/shard_map/reduce_scatter | solution.py:251
  835.5 276.8 %reduce-scatter.20.cloned.1.call-start = ((), (), s32[]{:S(2)}) async-start(), calls=%async_computation.26 | async-start | bytes 8912896 | tf_op jit(solution)/shard_map/reduce_scatter | solution.py:249
  841.1 379.0 %reduce-scatter.26.cloned.1.call-start = ((), (), s32[]{:S(2)}) async-start(), calls=%async_computation.29 | async-start | bytes 8912896 | tf_op jit(solution)/shard_map/reduce_scatter | solution.py:252
  847.9 707.0 %reduce-scatter.28.cloned.1.call-start = ((), (), s32[]{:S(2)}) async-start(), calls=%async_computation.30 | async-start | bytes 35651584 | tf_op jit(solution)/shard_map/reduce_scatter | solution.py:253
  863.1 1026.3 %reduce-scatter.30.cloned.1.call-start = ((), (), s32[]{:S(2)}) async-start(), calls=%async_computation.31 | async-start | bytes 35651584 | tf_op jit(solution)/shard_map/reduce_scatter | solution.py:254
  878.0 1345.7 %reduce-scatter.32.cloned.1.call-start = ((), (), s32[]{:S(2)}) async-start(), calls=%async_computation.32 | async-start | bytes 35651584 | tf_op jit(solution)/shard_map/reduce_scatter | solution.py:255
  (35 other events, 664.9 us)
Sparse Core Ops, SparseCore 0:
  33.9 18.5 all-gather.13
  54.7 37.8 all-gather.17
  94.7 36.7 all-gather.15
  133.6 49.3 all-gather.19
  185.0 51.0 all-gather.21
  241.0 30.0 reduce-scatter.11
  274.2 21.2 all-gather.23
  297.7 126.4 all-gather.25
  426.3 124.5 all-gather.27
  552.3 19.4 all-gather.31
  574.0 129.8 all-gather.29
  742.6 30.0 reduce-scatter.15
  778.1 21.2 all-gather.33
  819.2 31.8 reduce-scatter.17
  853.8 20.3 reduce-scatter.13
  878.4 61.8 reduce-scatter.21
  944.5 60.7 reduce-scatter.23
  1009.8 102.3 reduce-scatter.19
  1116.9 103.2 reduce-scatter.25
  1224.8 330.1 reduce-scatter.27
  1559.8 329.5 reduce-scatter.29
  1894.3 329.3 reduce-scatter.31
where the time goes:
time: 2240 us; the launch traced here: 2230 us
  waiting for transfers between devices  1940 us (87%)
  matrix products  163 us (7%)
  blocking collectives  81.6 us (4%)
    reduce_scatter x1, waiting for transfers between devices, shards(): lax.psum_scatter(grad_gate, 'dp', scatter_dimension=0, tiled=True)  335 us
    reduce_scatter x1, waiting for transfers between devices, shards(): lax.psum_scatter(grad_up, 'dp', scatter_dimension=0, tiled=True)  334 us
    reduce_scatter x1, waiting for transfers between devices, shards(): lax.psum_scatter(grad_down, 'dp', scatter_dimension=1, tiled=True)  334 us
    all_gather x1, waiting for transfers between devices, shards(): lax.all_gather(down_weight, 'dp', axis=1, tiled=True)  132 us
    all_gather x1, waiting for transfers between devices, shards(): lax.all_gather(gate_weight, 'dp', axis=0, tiled=True)  129 us
    all_gather x1, waiting for transfers between devices, shards(): lax.all_gather(up_weight, 'dp', axis=0, tiled=True)  114 us
    reduce_scatter x1, waiting for transfers between devices, shards(): lax.psum_scatter(grad_out, 'dp', scatter_dimension=1, tiled=True)  108 us
    reduce_scatter x1, waiting for transfers between devices, shards(): lax.psum_scatter(grad_query, 'dp', scatter_dimension=0, tiled=True)  107 us
  transfers between devices with their start and end apart: 22, of which 19 were waited for; matrix products, arithmetic and copies ran while one was open for 5% of the time, Pallas kernels for 0%

commit v1 on v0

v1 whole, which is shorter than its diff:
```python
import math

import jax
import jax.numpy as jnp
import numpy as np
from jax import lax
from jax.experimental import pallas as pl
from jax.experimental.pallas import tpu as pltpu
from jax.sharding import PartitionSpec as P

HEAD_SIZE = 64


eps = 1e-05
rope_theta = 500000.0
f32 = jnp.float32
bf16 = jnp.bfloat16


def rope_table(head_dim):
    half_dim = head_dim // 2
    base_freq = 1.0 / rope_theta ** (np.arange(half_dim) * 2.0 / head_dim)
    wavelen = 2.0 * math.pi / base_freq
    smooth = (8192.0 / wavelen - 1.0) / 3.0
    middle = (1.0 - smooth) * base_freq / 32.0 + smooth * base_freq
    return np.where(
        wavelen > 8192.0, base_freq / 32.0, np.where(wavelen < 2048.0, base_freq, middle)
    )


def rotary_apply(heads, cosine_lookup, sine_lookup, turn):
    half_dim = heads.shape[-1] // 2
    cosine_part = cosine_lookup[:, None, :]
    sine_part = turn * sine_lookup[:, None, :]
    front_half = heads[..., :half_dim]
    back_half = heads[..., half_dim:]
    return jnp.concatenate(
        [
            front_half * cosine_part - back_half * sine_part,
            back_half * cosine_part + front_half * sine_part,
        ],
        axis=-1,
    )


def dot(left, right):
    return jnp.dot(left, right, preferred_element_type=f32)


def contract_rows(left, right):
    return lax.dot_general(left, right, (((0,), (0,)), ((), ())), preferred_element_type=f32)


def contract_cols(left, right):
    return lax.dot_general(left, right, (((1,), (1,)), ((), ())), preferred_element_type=f32)


def after(value, *earlier):
    return lax.optimization_barrier((value,) + earlier)[0]


class Axes:
    def __init__(self, dp):
        self.dp = dp
        self.n = dp // 4
        index = lax.axis_index("dp").astype(jnp.int32)
        self.z = index // 4
        self.x = (index // 2) % 2
        self.c = index % 2
        self.y = lax.axis_index("tp").astype(jnp.int32)

    def over_core(self, value):
        return lax.ppermute(value, "dp", [(i, i ^ 1) for i in range(self.dp)])

    def over_x(self, value):
        return lax.ppermute(value, "dp", [(i, i ^ 2) for i in range(self.dp)])

    def over_y(self, value):
        return lax.ppermute(value, "tp", [(0, 1), (1, 0)])

    def over_z(self, value, pairs):
        return lax.ppermute(
            value, "dp", [(a * 4 + low, b * 4 + low) for a, b in pairs for low in range(4)]
        )

    def across(self, step):
        return [(i, i ^ step) for i in range(self.n)]

    def gather_z(self, own):
        if self.n != 4:
            return [own] + [self.over_z(own, self.across(s)) for s in range(1, self.n)]
        one = self.over_z(own, self.across(1))
        three = self.over_z(own, [(1, 2), (2, 1)])
        two_out = self.over_z(three, [(1, 0), (2, 3)])
        two_in = self.over_z(one, [(1, 2), (2, 1)])
        three_out = self.over_z(two_in, [(1, 0), (2, 3)])
        return [own, one, two_out + two_in, three + three_out]

    def scatter_z(self, parts):
        if self.n != 4:
            total = parts[0].astype(f32)
            for s in range(1, self.n):
                total = total + self.over_z(parts[s].astype(bf16), self.across(s)).astype(f32)
            return total
        far = self.over_z(parts[3].astype(bf16), [(0, 1), (3, 2)])
        near = self.over_z(parts[2].astype(bf16), [(0, 1), (3, 2)])
        passed = (parts[2].astype(f32) + far.astype(f32)).astype(bf16)
        passed = self.over_z(passed, [(1, 2), (2, 1)])
        three = (parts[3].astype(f32) + near.astype(f32)).astype(bf16)
        three = self.over_z(three, [(1, 2), (2, 1)])
        one = (parts[1].astype(f32) + passed.astype(f32)).astype(bf16)
        one = self.over_z(one, self.across(1))
        return parts[0].astype(f32) + one.astype(f32) + three.astype(f32)

    def exchange_z(self, parts):
        return [parts[0]] + [self.over_z(parts[s], self.across(s)) for s in range(1, self.n)]

    def place_rows(self, parts):
        count = len(parts)
        rows, cols = parts[0].shape
        tile = min(cols, 512)

        def body(z_ref, *refs):
            for s in range(count):
                refs[-1][z_ref[0] ^ s] = refs[s][...]

        out = pl.pallas_call(
            body,
            out_shape=jax.ShapeDtypeStruct((count, rows, cols), parts[0].dtype),
            grid_spec=pltpu.PrefetchScalarGridSpec(
                num_scalar_prefetch=1,
                grid=(cols // tile,),
                in_specs=[pl.BlockSpec((rows, tile), lambda i, z: (0, i))] * count,
                out_specs=pl.BlockSpec((count, rows, tile), lambda i, z: (0, 0, i)),
            ),
            name="place_rows",
        )(self.z.reshape(1), *parts)
        return out.reshape(count * rows, cols)

    def gather_rows(self, own):
        parts = self.gather_z(own)
        here = self.place_rows(parts)
        there = self.place_rows([self.over_x(part) for part in parts])
        return [here, there, self.over_core(here), self.over_core(there)]

    def reduce_rows(self, left, right):
        width = left.shape[1]
        half, quarter = width // 2, width // 4
        away = contract_rows(left[:, half:], right).astype(bf16)
        got = self.over_core(away)
        beside = (contract_rows(left[:, quarter:half], right) + got[quarter:].astype(f32)).astype(bf16)
        beside_got = self.over_x(beside)
        here = (
            contract_rows(left[:, :quarter], right)
            + got[:quarter].astype(f32)
            + beside_got.astype(f32)
        ).astype(bf16)
        here = here.reshape(self.n, quarter // self.n, right.shape[1])
        return [
            lax.dynamic_index_in_dim(here, self.z ^ s, 0, keepdims=False) for s in range(self.n)
        ]


def finish_ffn(axes, both, down, gain, gate_weight, up_weight):
    count = len(both)
    rows = both[0].shape[0]
    width = both[0].shape[1] // 2

    def body(z_ref, gain_ref, gate_w, up_w, *refs):
        both_refs, down_refs = refs[:count], refs[count : 2 * count]
        gate_out, up_out, down_out, gain_out = refs[2 * count :]
        scale = gain_ref[...]
        total = jnp.zeros((rows, 1), f32)
        for s in range(count):
            start = pl.multiple_of((z_ref[0] ^ s) * width, width)
            spot = pl.ds(start, width)
            gate_part = both_refs[s][:, :width].astype(f32)
            up_part = both_refs[s][:, width:].astype(f32)
            gate_out[:, spot] = gate_part * scale
            up_out[:, spot] = up_part * scale
            total = total + jnp.sum(
                gate_part * gate_w[:, spot].astype(f32) + up_part * up_w[:, spot].astype(f32),
                axis=1,
                keepdims=True,
            )
            down_out[spot, :] = down_refs[s][...].astype(f32).T
        gain_out[...] = total

    full = count * width
    memory = pl.BlockSpec(memory_space=pltpu.VMEM)
    return pl.pallas_call(
        body,
        out_shape=(
            jax.ShapeDtypeStruct((rows, full), f32),
            jax.ShapeDtypeStruct((rows, full), f32),
            jax.ShapeDtypeStruct((full, rows), f32),
            jax.ShapeDtypeStruct((rows, 1), f32),
        ),
        in_specs=[pl.BlockSpec(memory_space=pltpu.SMEM)] + [memory] * (3 + 2 * count),
        out_specs=(memory,) * 4,
        name="finish_ffn",
    )(axes.z.reshape(1), gain, gate_weight, up_weight, *both, *down)


def norm_back(value, inverse, grad):
    mean = jnp.mean(grad * value, axis=1, keepdims=True)
    return inverse * grad - value * (inverse * inverse * inverse * mean)


def shards(
    dp,
    tokens,
    gain_attn,
    query_weight,
    key_matrix,
    value_matrix,
    out_weight,
    gain_ffn,
    gate_weight,
    up_weight,
    down_weight,
    cotangent,
    seq_lens,
    pad_mask,
    positions,
):
    axes = Axes(dp)
    n = axes.n
    own_rows, width = tokens.shape
    block = width // dp
    group_rows = pad_mask.shape[0]
    query_cols = query_weight.shape[1]
    key_cols = key_matrix.shape[1]
    heads_kv = key_cols // HEAD_SIZE
    heads_query = query_cols // HEAD_SIZE
    group_size = heads_query // heads_kv
    score_scale = 1.0 / math.sqrt(HEAD_SIZE)
    hidden_cols = gate_weight.shape[1] // n
    quarter = width // 4

    place = jnp.arange(dp, dtype=jnp.int32)
    to_block = (place % n) * 4 + (((place // n) % 2) ^ axes.x) * 2 + ((place // (2 * n)) ^ axes.c)
    to_place = ((place % 2) ^ axes.c) * (2 * n) + (((place // 2) % 2) ^ axes.x) * n + place // 4

    def reorder(value, order):
        blocks = value.reshape(value.shape[0], dp, block)
        return jnp.take(blocks, order, axis=1, mode="clip").reshape(value.shape)

    scale_attn = gain_attn.astype(f32)[:, None]
    scale_ffn = gain_ffn.astype(f32)[:, None]
    own_qkv = jnp.concatenate([query_weight, key_matrix, value_matrix], axis=1)
    qkv_pieces = axes.gather_rows((own_qkv.astype(f32) * scale_attn).astype(bf16))
    out_pieces = axes.gather_rows(after(out_weight.T, qkv_pieces[0]))

    def hidden_part(weight, s):
        part = lax.dynamic_slice_in_dim(weight, (axes.z ^ s) * hidden_cols, hidden_cols, 1)
        return (part.astype(f32) * scale_ffn).astype(bf16)

    def down_part(s):
        return lax.dynamic_slice_in_dim(
            down_weight, (axes.z ^ s) * hidden_cols, hidden_cols, 0
        ).T

    def gather_hidden(parts):
        here = axes.place_rows(axes.exchange_z(parts))
        there = axes.over_x(here)
        return jnp.concatenate(
            [here, there, axes.over_core(here), axes.over_core(there)], axis=0
        )

    both_parts = [
        jnp.concatenate([hidden_part(gate_weight, s), hidden_part(up_weight, s)], axis=1)
        for s in range(n)
    ]
    down_parts = [down_part(s) for s in range(n)]
    both_full = gather_hidden([after(part, out_pieces[0]) for part in both_parts])
    down_full = gather_hidden([after(part, both_full) for part in down_parts])

    inputs_wide = reorder(tokens, to_block).astype(f32)
    cotangent_low = reorder(cotangent, to_block)
    inverse_one = lax.rsqrt(jnp.mean(inputs_wide * inputs_wide, axis=1, keepdims=True) + eps)
    normed_one = (inputs_wide * inverse_one).astype(bf16)

    def pair_rows(own):
        return jnp.concatenate([own, axes.over_y(own)], axis=0)

    def pair_of(vector):
        halves = vector.reshape(2, own_rows)
        return jnp.concatenate([jnp.take(halves, axes.y, axis=0), jnp.take(halves, 1 - axes.y, axis=0)])

    normed_one_all = pair_rows(normed_one)

    def columns(value, piece):
        return value[:, piece * quarter : (piece + 1) * quarter]

    qkv = sum(dot(columns(normed_one_all, i), qkv_pieces[i]) for i in range(4))
    slot_ids = pair_of(jnp.arange(group_rows, dtype=jnp.int32))
    live_mask = pair_of(pad_mask)
    inverse_freq = jnp.asarray(rope_table(HEAD_SIZE), f32)
    angles = pair_of(positions).astype(f32)[:, None] * inverse_freq[None, :]
    cosine_lookup = jnp.cos(angles)
    sine_lookup = jnp.sin(angles)
    query_head_split = rotary_apply(
        qkv[:, :query_cols].reshape(group_rows, heads_query, HEAD_SIZE),
        cosine_lookup,
        sine_lookup,
        1.0,
    )
    query_head_split = query_head_split.astype(bf16).reshape(
        group_rows, heads_kv, group_size, HEAD_SIZE
    )
    key_head_split = rotary_apply(
        qkv[:, query_cols : query_cols + key_cols].reshape(group_rows, heads_kv, HEAD_SIZE),
        cosine_lookup,
        sine_lookup,
        1.0,
    ).astype(bf16)
    value_head_split = (
        qkv[:, query_cols + key_cols :].astype(bf16).reshape(group_rows, heads_kv, HEAD_SIZE)
    )
    segment = (slot_ids >= seq_lens[0]).astype(jnp.int32)
    allowed = (
        (segment[:, None] == segment[None, :])
        & (slot_ids[None, :] <= slot_ids[:, None])
        & ((live_mask[None, :] == 1) | (slot_ids[:, None] == slot_ids[None, :]))
    )
    scores = (
        jnp.einsum("qgmd,kgd->gmqk", query_head_split, key_head_split, preferred_element_type=f32)
        * score_scale
    )
    scores = jnp.where(allowed[None, None], scores, -1e30)
    row_peak = jnp.max(scores, axis=-1, keepdims=True)
    log_total = row_peak + jnp.log(jnp.sum(jnp.exp(scores - row_peak), axis=-1, keepdims=True))
    probs_low = jnp.exp(scores - log_total).astype(bf16)
    attended = jnp.einsum("gmqk,kgd->qgmd", probs_low, value_head_split, preferred_element_type=f32)
    attended = attended.reshape(group_rows, heads_query * HEAD_SIZE).astype(bf16)

    def split_sum(pieces):
        sent = jnp.concatenate([piece(slice(own_rows, None)) for piece in pieces], axis=1)
        got = axes.over_y(sent.astype(bf16))
        kept = jnp.concatenate([piece(slice(0, own_rows)) for piece in pieces], axis=1)
        return kept + got.astype(f32)

    branch = split_sum(
        [lambda rows, i=i: contract_cols(attended[rows], out_pieces[i]) for i in range(4)]
    )
    resid = inputs_wide + branch
    inverse_two = lax.rsqrt(jnp.mean(resid * resid, axis=1, keepdims=True) + eps)
    normed_two = (resid * inverse_two).astype(bf16)

    def gather_tokens(own):
        parts = axes.gather_z(own)
        return jnp.concatenate(parts + [axes.over_y(part) for part in parts], axis=0)

    normed_two_all = gather_tokens(normed_two)
    cotangent_all = gather_tokens(after(cotangent_low, normed_two_all))
    line_rows = n * own_rows
    gate_up = dot(normed_two_all, both_full)
    gate_proj, up_proj = gate_up[:, :hidden_cols], gate_up[:, hidden_cols:]
    sigmoid_gate = jax.nn.sigmoid(gate_proj)
    gate_active = gate_proj * sigmoid_gate
    hidden = (gate_active * up_proj).astype(bf16)
    hidden_grad = dot(cotangent_all, down_full)
    gate_grad = (
        hidden_grad * up_proj * sigmoid_gate * (1.0 + gate_proj * (1.0 - sigmoid_gate))
    ).astype(bf16)
    up_grad = (hidden_grad * gate_active).astype(bf16)
    both_grad = jnp.concatenate([gate_grad, up_grad], axis=1)

    def scatter_tokens(left, right):
        sent = contract_cols(left[line_rows:], right).astype(bf16)
        got = [
            axes.over_y(sent[s * own_rows : (s + 1) * own_rows]) for s in range(n)
        ]
        kept = contract_cols(left[:line_rows], right)
        return axes.scatter_z(
            [
                kept[s * own_rows : (s + 1) * own_rows] + got[s].astype(f32)
                for s in range(n)
            ]
        )

    normed_two_grad = scatter_tokens(both_grad, both_full)
    branch_feed = scatter_tokens(after(hidden, normed_two_grad), down_full)
    output = reorder((resid + branch_feed).astype(bf16), to_place)

    down_sums = axes.reduce_rows(cotangent_all, hidden)
    both_sums = axes.reduce_rows(normed_two_all, both_grad)
    down_got = axes.exchange_z(down_sums)
    both_got = axes.exchange_z(both_sums)
    grad_gate, grad_up, grad_down, gain_two_sum = finish_ffn(
        axes, both_got, down_got, scale_ffn, gate_weight, up_weight
    )

    resid_grad = cotangent_low.astype(f32) + norm_back(resid, inverse_two, normed_two_grad)
    resid_low_all = pair_rows(resid_grad.astype(bf16))
    attended_grad = sum(dot(columns(resid_low_all, i), out_pieces[i]) for i in range(4))
    out_sum = axes.scatter_z(axes.reduce_rows(resid_low_all, attended))
    attended_heads = attended_grad.astype(bf16).reshape(
        group_rows, heads_kv, group_size, HEAD_SIZE
    )
    probs_full = jnp.exp(scores - log_total)
    prob_grad = jnp.einsum(
        "qgmd,kgd->gmqk", attended_heads, value_head_split, preferred_element_type=f32
    )
    row_delta = jnp.sum(prob_grad * probs_full, axis=-1, keepdims=True)
    score_grad = (probs_full * (prob_grad - row_delta)).astype(bf16)
    value_grad = jnp.einsum("gmqk,qgmd->kgd", probs_low, attended_heads, preferred_element_type=f32)
    value_grad = value_grad.reshape(group_rows, key_cols).astype(bf16)
    query_grad = (
        jnp.einsum("gmqk,kgd->qgmd", score_grad, key_head_split, preferred_element_type=f32)
        * score_scale
    )
    query_grad = rotary_apply(
        query_grad.reshape(group_rows, heads_query, HEAD_SIZE), cosine_lookup, sine_lookup, -1.0
    )
    query_grad = query_grad.reshape(group_rows, query_cols).astype(bf16)
    key_grad = (
        jnp.einsum("gmqk,qgmd->kgd", score_grad, query_head_split, preferred_element_type=f32)
        * score_scale
    )
    key_grad = (
        rotary_apply(key_grad, cosine_lookup, sine_lookup, -1.0)
        .reshape(group_rows, key_cols)
        .astype(bf16)
    )
    qkv_grad = jnp.concatenate([query_grad, key_grad, value_grad], axis=1)
    normed_one_grad = split_sum(
        [lambda rows, i=i: contract_cols(qkv_grad[rows], qkv_pieces[i]) for i in range(4)]
    )
    qkv_sum = axes.scatter_z(axes.reduce_rows(normed_one_all, qkv_grad))
    token_grad = reorder(
        resid_grad + norm_back(inputs_wide, inverse_one, normed_one_grad), to_place
    )
    gain_one_sum = jnp.sum(qkv_sum * own_qkv.astype(f32), axis=1)
    qkv_out = qkv_sum * scale_attn

    def share(vector):
        total = vector + axes.over_y(vector)
        return lax.dynamic_slice_in_dim(total, axes.y * (block // 2), block // 2)

    return (
        output,
        token_grad,
        share(gain_one_sum),
        qkv_out[:, :query_cols],
        qkv_out[:, query_cols : query_cols + key_cols],
        qkv_out[:, query_cols + key_cols :],
        out_sum.T,
        share(gain_two_sum[:, 0]),
        grad_gate,
        grad_up,
        grad_down,
    )


def solution(mesh):
    dp = mesh.shape["dp"]
    placed = (
        P(("dp", "tp"), None),
        P("dp"),
        P("dp", "tp"),
        P("dp", "tp"),
        P("dp", "tp"),
        P("tp", "dp"),
        P("dp"),
        P("dp", "tp"),
        P("dp", "tp"),
        P("tp", "dp"),
        P(("dp", "tp"), None),
        P("dp"),
        P("dp"),
        P("dp"),
    )

    def program(*arrays):
        return shards(dp, *arrays)

    return jax.shard_map(
        program,
        mesh=mesh,
        in_specs=placed,
        out_specs=(
            P(("dp", "tp"), None),
            P(("dp", "tp"), None),
            P(("dp", "tp")),
            P("dp", "tp"),
            P("dp", "tp"),
            P("dp", "tp"),
            P("tp", "dp"),
            P(("dp", "tp")),
            P("dp", "tp"),
            P("dp", "tp"),
            P("tp", "dp"),
        ),
        check_vma=False,
    )
```

time: 2240 us -> 714 us (0.32)
  waiting for transfers between devices: 1940 us -> 256 us
  starting transfers between devices: 1.81 us -> 185 us
  blocking collectives: 81.6 us -> 0 us
  other arithmetic: 19.9 us -> 65 us
  local copies, waits for them, and re-layouts: 10.9 us -> 48.5 us
  matrix products: 163 us -> 127 us
  Pallas kernels: 0 us -> 23.3 us
    reduce_scatter x11 -> x0, waiting for transfers between devices: 1320 us -> none  [the longest x1 335 us: shards(): lax.psum_scatter(grad_gate, 'dp', scatter_dimension=0, tiled=True)]
    all_gather x11 -> x0, waiting for transfers between devices: 608 us -> none  [the longest x1 132 us: shards(): lax.all_gather(down_weight, 'dp', axis=1, tiled=True)]
    ppermute x0 -> x100, waiting for transfers between devices: none -> 256 us  [the longest x52 128 us: over_z(): lax.ppermute(value, 'dp', [(a * 4 + low, b * 4 + low) for a, b in pairs f...]
    ppermute x0 -> x100, starting transfers between devices: none -> 185 us  [the longest x52 148 us: over_z(): lax.ppermute(value, 'dp', [(a * 4 + low, b * 4 + low) for a, b in pairs f...]
    all_gather x2 -> x0, blocking collectives: 41.8 us -> none  [the longest x1 23.3 us: shards(): lax.all_gather(gain_attn, 'dp', axis=0, tiled=True)]
    unnamed x1 -> x0, blocking collectives: 39.8 us -> none
    dot_general x7 -> x12, matrix products: 60.3 us -> 32.7 us  [contract_rows(): lax.dot_general(left, right, (((0,), (0,)), ((), ())), preferred_element_...]
    pallas_call x0 -> x7, Pallas kernels: none -> 23.3 us  [the longest x6 17.2 us: place_rows(): pl.pallas_call(body, out_shape=jax.ShapeDtypeStruct((count, rows, cols),...]
  transfers between devices with their start and end apart: 22 -> 100, of which waited for: 19 -> 37; matrix products, arithmetic and copies ran while one was open for 5% -> 30% of each run, Pallas kernels for 0% -> 3%
where the time goes in v1:
time: 714 us; the launch traced here: 708 us
  waiting for transfers between devices  256 us (36%)
  starting transfers between devices  185 us (26%)
  matrix products  127 us (18%)
  other arithmetic  65 us (9%)
  local copies, waits for them, and re-layouts  48.5 us (7%)
  Pallas kernels  23.3 us (3%)
    ppermute x52, starting transfers between devices, over_z(): lax.ppermute(value, 'dp', [(a * 4 + low, b * 4 + low) for a, b in pairs f...  148 us
    ppermute x52, waiting for transfers between devices, over_z(): lax.ppermute(value, 'dp', [(a * 4 + low, b * 4 + low) for a, b in pairs f...  128 us
    ppermute x14, waiting for transfers between devices, over_x(): return lax.ppermute(value, 'dp', [(i, i ^ 2) for i in range(self.dp)])  67.2 us
    ppermute x22, waiting for transfers between devices, over_y(): return lax.ppermute(value, 'tp', [(0, 1), (1, 0)])  60.7 us
    dot_general x20, matrix products, contract_cols(): lax.dot_general(left, right, (((1,), (1,)), ((), ())), preferred_element_...  47.9 us
    dot_general x10, matrix products, dot(): return jnp.dot(left, right, preferred_element_type=f32)  38.3 us
    dot_general x12, matrix products, contract_rows(): lax.dot_general(left, right, (((0,), (0,)), ((), ())), preferred_element_...  32.7 us
    unnamed x232, local copies, waits for them, and re-layouts  24.9 us
  transfers between devices with their start and end apart: 100, of which 37 were waited for; matrix products, arithmetic and copies ran while one was open for 30% of the time, Pallas kernels for 3%

profile of v1, /device:TPU:0, one launch (start us, length us, event | category | flops | bytes accessed | tf_op | source)
XLA Modules:
  0.0 708.2 jit_solution(17959968936050336941)
XLA Ops:
  20.6 10.8 %collective-permute-done.3 = bf16[128,1536]{1,0:T(8,128)(2,1)} collective-permute-done((bf16[128,1536]{1,0:T(8,128)(2,1)S(1)}, bf16[128,1536]{1,0:T(8,128)(2,1)}, u32[]{:S(2)}, u32[]{:S(2)}) %collective-permute-start.3) | collective-permute-done | bytes 393248 | tf_op jit(solution)/shard_map/ppermute | solution.py:82
  69.0 7.3 %collective-permute-done.16 = bf16[128,1024]{1,0:T(8,128)(2,1)S(1)} collective-permute-done((bf16[128,1024]{1,0:T(8,128)(2,1)}, bf16[128,1024]{1,0:T(8,128)(2,1)S(1)}, u32[]{:S(2)}, u32[]{:S(2)}) %collective-permute-start.16) | collective-permute-done | bytes 262176 | tf_op jit(solution)/shard_map/ppermute | solution.py:82
  103.5 26.0 %collective-permute-done.34.refs_2_ = bf16[128,2048]{1,0:T(8,128)(2,1)} collective-permute-done((bf16[128,2048]{1,0:T(8,128)(2,1)}, bf16[128,2048]{1,0:T(8,128)(2,1)}, u32[]{:S(2)}, u32[]{:S(2)}) %collective-permute-start.34) | collective-permute-done | bytes 524320 | tf_op jit(solution)/shard_map/ppermute | solution.py:82
  155.2 10.4 %collective-permute-done.23 = bf16[128,2048]{1,0:T(8,128)(2,1)S(1)} collective-permute-done((bf16[128,2048]{1,0:T(8,128)(2,1)S(1)}, bf16[128,2048]{1,0:T(8,128)(2,1)S(1)}, u32[]{:S(2)}, u32[]{:S(2)}) %collective-permute-start.23) | collective-permute-done | bytes 524320 | tf_op jit(solution)/shard_map/ppermute | solution.py:79
  173.0 8.0 %collective-permute-done.24 = bf16[128,2048]{1,0:T(8,128)(2,1)} collective-permute-done((bf16[128,2048]{1,0:T(8,128)(2,1)}, bf16[128,2048]{1,0:T(8,128)(2,1)}, u32[]{:S(2)}, u32[]{:S(2)}) %collective-permute-start.24) | collective-permute-done | bytes 524320 | tf_op jit(solution)/shard_map/ppermute | solution.py:82
  199.0 8.4 %collective-permute-done.28 = bf16[128,2048]{1,0:T(8,128)(2,1)S(1)} collective-permute-done((bf16[128,2048]{1,0:T(8,128)(2,1)}, bf16[128,2048]{1,0:T(8,128)(2,1)S(1)}, u32[]{:S(2)}, u32[]{:S(2)}) %collective-permute-start.28) | collective-permute-done | bytes 524320 | tf_op jit(solution)/shard_map/ppermute | solution.py:82
  213.1 9.7 %collective-permute-done.31 = bf16[128,2048]{1,0:T(8,128)(2,1)S(1)} collective-permute-done((bf16[128,2048]{1,0:T(8,128)(2,1)S(1)}, bf16[128,2048]{1,0:T(8,128)(2,1)S(1)}, u32[]{:S(2)}, u32[]{:S(2)}) %collective-permute-start.31) | collective-permute-done | bytes 524320 | tf_op jit(solution)/shard_map/ppermute | solution.py:79
  223.6 9.8 %collective-permute-done.32 = bf16[128,2048]{1,0:T(8,128)(2,1)S(1)} collective-permute-done((bf16[128,2048]{1,0:T(8,128)(2,1)S(1)}, bf16[128,2048]{1,0:T(8,128)(2,1)S(1)}, u32[]{:S(2)}, u32[]{:S(2)}) %collective-permute-start.32) | collective-permute-done | bytes 524320 | tf_op jit(solution)/shard_map/ppermute | solution.py:79
  251.3 7.0 pad_maximum_fusion
  270.0 22.7 %collective-permute-done.49.refs_2_ = bf16[128,1024]{1,0:T(8,128)(2,1)} collective-permute-done((bf16[128,1024]{1,0:T(8,128)(2,1)S(1)}, bf16[128,1024]{1,0:T(8,128)(2,1)}, u32[]{:S(2)}, u32[]{:S(2)}) %collective-permute-start.49) | collective-permute-done | bytes 262176 | tf_op jit(solution)/shard_map/ppermute | solution.py:82
  296.5 14.6 %fusion.165 = f32[1024,2048]{1,0:T(8,128)} fusion(bf16[1024,2048]{1,0:T(8,128)(2,1)} %constant_dynamic-update-slice_fusion, bf16[2048,2048]{1,0:T(8,128)(2,1)} %pad_maximum_fusion), kind=kOutput, calls=%fused_computation.356 | convolution fusion | flops 8589934592 | bytes 20971520 | tf_op jit(solution)/shard_map/dot_general | solution.py:47
  323.5 11.2 %collective-permute-done.47 = bf16[128,2048]{1,0:T(8,128)(2,1)S(1)} collective-permute-done((bf16[128,2048]{1,0:T(8,128)(2,1)S(1)}, bf16[128,2048]{1,0:T(8,128)(2,1)S(1)}, u32[]{:S(2)}, u32[]{:S(2)}) %collective-permute-start.47) | collective-permute-done | bytes 524320 | tf_op jit(solution)/shard_map/ppermute | solution.py:79
  334.8 12.2 %multiply_convert_fusion = (bf16[1024,1024]{1,0:T(8,128)(2,1)}, bf16[1024,1024]{1,0:T(8,128)(2,1)}, bf16[1024,1024]{1,0:T(8,128)(2,1)S(1)}) fusion(f32[1024,2048]{1,0:T(8,128)} %fusion.165, bf16[1024,2048]{1,0:T(8,128)(2,1)S(1)} %constant_dynamic-update-slice_fusion.8, bf16[512,1024]{1,0:T(8,128)(2,1)S(1)} %collective-permute-done.53, ...), kind=kOutput, calls=%fused_computation.19 | convolution fusion | flops 4327473152 | bytes 23068672 | tf_op jit(solution)/shard_map/dot_general | solution.py:47
  347.1 6.8 convolution_convert_fusion.3
  369.1 6.8 collective-permute-start.58
  417.3 6.8 convolution_convert_fusion.2
  425.9 8.4 %fusion.52 = f32[512,2048]{1,0:T(8,128)} fusion(bf16[1024,1024]{1,0:T(8,128)(2,1)S(1)} %get-tuple-element.37, bf16[512,1024]{1,0:T(8,128)(2,1)S(1)} %copy-done.98, bf16[512,1024]{1,0:T(8,128)(2,1)S(1)} %copy-done.96, bf16[512,1024]{1,0:T(8,128)(2,1)S(1)} %copy-done.94, bf16[512,1024]{1,0:T(8,128)(2,1)S(1)} %bitcast.325), kind=kOutput, calls=%fused_computation.132 | convolution fusion | flops 2164260864 | bytes 9437184 | tf_op jit(solution)/shard_map/dot_general | solution.py:55
  467.9 9.3 %collective-permute-done.73 = bf16[128,2048]{1,0:T(8,128)(2,1)S(1)} collective-permute-done((bf16[128,2048]{1,0:T(8,128)(2,1)S(1)}, bf16[128,2048]{1,0:T(8,128)(2,1)S(1)}, u32[]{:S(2)}, u32[]{:S(2)}) %collective-permute-start.73) | collective-permute-done | bytes 524320 | tf_op jit(solution)/shard_map/ppermute | solution.py:79
  494.2 6.8 collective-permute-start.70
  509.4 8.7 %collective-permute-done.83 = bf16[512,1024]{1,0:T(8,128)(2,1)S(1)} collective-permute-done((bf16[512,1024]{1,0:T(8,128)(2,1)S(1)}, bf16[512,1024]{1,0:T(8,128)(2,1)S(1)}, u32[]{:S(2)}, u32[]{:S(2)}) %collective-permute-start.83) | collective-permute-done | bytes 1048608 | tf_op jit(solution)/shard_map/ppermute | solution.py:76
  556.6 37.0 %collective-permute-done.90 = bf16[512,2048]{1,0:T(8,128)(2,1)} collective-permute-done((bf16[512,2048]{1,0:T(8,128)(2,1)}, bf16[512,2048]{1,0:T(8,128)(2,1)}, u32[]{:S(2)}, u32[]{:S(2)}) %collective-permute-start.90) | collective-permute-done | bytes 2097184 | tf_op jit(solution)/shard_map/ppermute | solution.py:76
  603.7 11.9 %collective-permute-start.79 = (bf16[128,1536]{1,0:T(8,128)(2,1)S(1)}, bf16[128,1536]{1,0:T(8,128)(2,1)S(1)}, u32[]{:S(2)}, u32[]{:S(2)}) collective-permute-start(bf16[128,1536]{1,0:T(8,128)(2,1)S(1)} %get-tuple-element.65), channel_id=1, source_target_pairs={{0,8},{2,10},{4,12},{6,14},{24,16},{26,18},{28,20},{30,22},{1,9},{... | collective-permute-start | bytes 1179656 | tf_op jit(solution)/shard_map/ppermute | solution.py:82
  630.7 9.2 %collective-permute-done.69 = bf16[128,2048]{1,0:T(8,128)(2,1)S(1)} collective-permute-done((bf16[128,2048]{1,0:T(8,128)(2,1)S(1)}, bf16[128,2048]{1,0:T(8,128)(2,1)S(1)}, u32[]{:S(2)}, u32[]{:S(2)}) %collective-permute-start.69) | collective-permute-done | bytes 524320 | tf_op jit(solution)/shard_map/ppermute | solution.py:82
  639.9 39.2 %collective-permute-start.86 = (bf16[128,1024]{0,1:T(8,128)(2,1)}, bf16[128,1024]{0,1:T(8,128)(2,1)}, u32[]{:S(2)}, u32[]{:S(2)}) collective-permute-start(bf16[128,1024]{0,1:T(8,128)(2,1)} %fusion.65), channel_id=1, source_target_pairs={{0,8},{2,10},{4,12},{6,14},{8,0},{10,2},{12,4},{14,6},{16,24},{18,... | collective-permute-start | bytes 786440 | tf_op jit(solution)/shard_map/ppermute | solution.py:82
  (570 shorter events, 395.6 us)
Async XLA Ops:
  2.5 42.1 %collective-permute-start.6 = (bf16[128,1536]{1,0:T(8,128)(2,1)S(1)}, bf16[128,1536]{1,0:T(8,128)(2,1)}, u32[]{:S(2)}, u32[]{:S(2)}) collective-permute-start(bf16[128,1536]{1,0:T(8,128)(2,1)S(1)} %fusion.54.refs_0_), channel_id=1, source_target_pairs={{0,4},{2,6},{4,0},{6,2},{8,12},{10,14},{12,8},{14,10},{16,20},{18,... | collective-permute-start | bytes 1179656 | tf_op jit(solution)/shard_map/ppermute | solution.py:76
  49.3 85.1 %collective-permute-start.10 = (bf16[512,1536]{1,0:T(8,128)(2,1)S(1)}, bf16[512,1536]{1,0:T(8,128)(2,1)}, u32[]{:S(2)}, u32[]{:S(2)}) collective-permute-start(bf16[512,1536]{1,0:T(8,128)(2,1)S(1)} %bitcast.260), channel_id=1, source_target_pairs={{0,2},{2,0},{4,6},{6,4},{8,10},{10,8},{12,14},{14,12},{16,18},{18,... | collective-permute-start | bytes 4718600 | tf_op jit(solution)/shard_map/ppermute | solution.py:73
  57.7 78.6 %collective-permute-start.11 = (bf16[512,1536]{1,0:T(8,128)(2,1)}, bf16[512,1536]{1,0:T(8,128)(2,1)}, u32[]{:S(2)}, u32[]{:S(2)}) collective-permute-start(bf16[512,1536]{1,0:T(8,128)(2,1)} %bitcast.264), channel_id=1, source_target_pairs={{0,2},{2,0},{4,6},{6,4},{8,10},{10,8},{12,14},{14,12},{16,18},{18,... | collective-permute-start | bytes 4718600 | tf_op jit(solution)/shard_map/ppermute | solution.py:73
  103.5 43.1 %collective-permute-start.21 = (bf16[512,1024]{1,0:T(8,128)(2,1)}, bf16[512,1024]{1,0:T(8,128)(2,1)}, u32[]{:S(2)}, u32[]{:S(2)}) collective-permute-start(bf16[512,1024]{1,0:T(8,128)(2,1)} %bitcast.268), channel_id=1, source_target_pairs={{0,2},{2,0},{4,6},{6,4},{8,10},{10,8},{12,14},{14,12},{16,18},{18,... | collective-permute-start | bytes 3145736 | tf_op jit(solution)/shard_map/ppermute | solution.py:73
  133.4 55.8 %collective-permute-start.36 = (bf16[512,2048]{1,0:T(8,128)(2,1)}, bf16[512,2048]{1,0:T(8,128)(2,1)}, u32[]{:S(2)}, u32[]{:S(2)}) collective-permute-start(bf16[512,2048]{1,0:T(8,128)(2,1)} %bitcast.283), channel_id=1, source_target_pairs={{0,4},{2,6},{4,0},{6,2},{8,12},{10,14},{12,8},{14,10},{16,20},{18,... | collective-permute-start | bytes 6291464 | tf_op jit(solution)/shard_map/ppermute | solution.py:76
  185.1 66.1 %collective-permute-start.37 = (bf16[512,2048]{1,0:T(8,128)(2,1)}, bf16[512,2048]{1,0:T(8,128)(2,1)}, u32[]{:S(2)}, u32[]{:S(2)}) collective-permute-start(bf16[512,2048]{1,0:T(8,128)(2,1)} %bitcast.284), channel_id=1, source_target_pairs={{0,2},{2,0},{4,6},{6,4},{8,10},{10,8},{12,14},{14,12},{16,18},{18,... | collective-permute-start | bytes 6291464 | tf_op jit(solution)/shard_map/ppermute | solution.py:73
  196.9 54.4 %collective-permute-start.38 = (bf16[512,2048]{1,0:T(8,128)(2,1)}, bf16[512,2048]{1,0:T(8,128)(2,1)}, u32[]{:S(2)}, u32[]{:S(2)}) collective-permute-start(bf16[512,2048]{1,0:T(8,128)(2,1)} %collective-permute-done.36), channel_id=1, source_target_pairs={{0,2},{2,0},{4,6},{6,4},{8,10},{10,8},{12,14},{14,12},{16,18},{18,... | collective-permute-start | bytes 6291464 | tf_op jit(solution)/shard_map/ppermute | solution.py:73
  266.6 54.0 %collective-permute-start.44 = (bf16[128,2048]{1,0:T(8,128)(2,1)S(1)}, bf16[128,2048]{1,0:T(8,128)(2,1)}, u32[]{:S(2)}, u32[]{:S(2)}) collective-permute-start(bf16[128,2048]{1,0:T(8,128)(2,1)S(1)} %copy_bitcast_fusion.1), channel_id=1, source_target_pairs={{0,1},{1,0},{2,3},{3,2},{4,5},{5,4},{6,7},{7,6},{8,9},{9,8},{10,11... | collective-permute-start | bytes 1572872 | tf_op jit(solution)/shard_map/ppermute | solution.py:79
  267.2 55.1 %collective-permute-start.45 = (bf16[128,2048]{1,0:T(8,128)(2,1)}, bf16[128,2048]{1,0:T(8,128)(2,1)}, u32[]{:S(2)}, u32[]{:S(2)}) collective-permute-start(bf16[128,2048]{1,0:T(8,128)(2,1)} %collective-permute-done.39), channel_id=1, source_target_pairs={{0,1},{1,0},{2,3},{3,2},{4,5},{5,4},{6,7},{7,6},{8,9},{9,8},{10,11... | collective-permute-start | bytes 1572872 | tf_op jit(solution)/shard_map/ppermute | solution.py:79
  268.7 42.3 %collective-permute-start.41 = (bf16[128,2048]{1,0:T(8,128)(2,1)}, bf16[128,2048]{1,0:T(8,128)(2,1)}, u32[]{:S(2)}, u32[]{:S(2)}) collective-permute-start(bf16[128,2048]{1,0:T(8,128)(2,1)} %collective-permute-done.40), channel_id=1, source_target_pairs={{8,0},{10,2},{12,4},{14,6},{16,24},{18,26},{20,28},{22,30},{9,1},{... | collective-permute-start | bytes 1572872 | tf_op jit(solution)/shard_map/ppermute | solution.py:82
  408.8 93.9 %collective-permute-start.89 = (bf16[1024,2048]{1,0:T(8,128)(2,1)}, bf16[1024,2048]{1,0:T(8,128)(2,1)}, u32[]{:S(2)}, u32[]{:S(2)}) collective-permute-start(bf16[1024,2048]{1,0:T(8,128)(2,1)} %convolution_convert_fusion.1), channel_id=1, source_target_pairs={{0,2},{2,0},{4,6},{6,4},{8,10},{10,8},{12,14},{14,12},{16,18},{18,... | collective-permute-start | bytes 12582920 | tf_op jit(solution)/shard_map/ppermute | solution.py:73
  411.1 56.2 %collective-permute-start.95 = (bf16[512,1024]{1,0:T(8,128)(2,1)}, bf16[512,1024]{1,0:T(8,128)(2,1)}, u32[]{:S(2)}, u32[]{:S(2)}) collective-permute-start(bf16[512,1024]{1,0:T(8,128)(2,1)} %add_convert_fusion.3), channel_id=1, source_target_pairs={{0,4},{2,6},{4,0},{6,2},{8,12},{10,14},{12,8},{14,10},{16,20},{18,... | collective-permute-start | bytes 3145736 | tf_op jit(solution)/shard_map/ppermute | solution.py:76
  453.2 41.0 %collective-permute-start.74 = (bf16[1024,1536]{1,0:T(8,128)(2,1)S(1)}, bf16[1024,1536]{1,0:T(8,128)(2,1)S(1)}, u32[]{:S(2)}, u32[]{:S(2)}) collective-permute-start(bf16[1024,1536]{1,0:T(8,128)(2,1)S(1)} %convolution_convert_fusion), channel_id=1, source_target_pairs={{0,2},{2,0},{4,6},{6,4},{8,10},{10,8},{12,14},{14,12},{16,18},{18,... | collective-permute-start | bytes 9437192 | tf_op jit(solution)/shard_map/ppermute | solution.py:73
  502.7 49.2 %collective-permute-start.75 = (bf16[512,1536]{1,0:T(8,128)(2,1)}, bf16[512,1536]{1,0:T(8,128)(2,1)}, u32[]{:S(2)}, u32[]{:S(2)}) collective-permute-start(bf16[512,1536]{1,0:T(8,128)(2,1)} %fusion.6), channel_id=1, source_target_pairs={{0,4},{2,6},{4,0},{6,2},{8,12},{10,14},{12,8},{14,10},{16,20},{18,... | collective-permute-start | bytes 4718600 | tf_op jit(solution)/shard_map/ppermute | solution.py:76
  518.1 75.5 %collective-permute-start.90 = (bf16[512,2048]{1,0:T(8,128)(2,1)}, bf16[512,2048]{1,0:T(8,128)(2,1)}, u32[]{:S(2)}, u32[]{:S(2)}) collective-permute-start(bf16[512,2048]{1,0:T(8,128)(2,1)} %add_convert_fusion.1), channel_id=1, source_target_pairs={{0,4},{2,6},{4,0},{6,2},{8,12},{10,14},{12,8},{14,10},{16,20},{18,... | collective-permute-start | bytes 6291464 | tf_op jit(solution)/shard_map/ppermute | solution.py:76
  523.8 93.7 %collective-permute-start.63 = (bf16[128,2048]{1,0:T(8,128)(2,1)}, bf16[128,2048]{1,0:T(8,128)(2,1)}, u32[]{:S(2)}, u32[]{:S(2)}) collective-permute-start(bf16[128,2048]{1,0:T(8,128)(2,1)} %get-tuple-element.97), channel_id=1, source_target_pairs={{0,1},{1,0},{2,3},{3,2},{4,5},{5,4},{6,7},{7,6},{8,9},{9,8},{10,11... | collective-permute-start | bytes 1572872 | tf_op jit(solution)/shard_map/ppermute | solution.py:79
  537.9 80.3 %collective-permute-start.96 = (bf16[128,1024]{1,0:T(8,128)(2,1)}, bf16[128,1024]{1,0:T(8,128)(2,1)S(1)}, u32[]{:S(2)}, u32[]{:S(2)}) collective-permute-start(bf16[128,1024]{1,0:T(8,128)(2,1)} %get-tuple-element.119), channel_id=1, source_target_pairs={{0,8},{2,10},{4,12},{6,14},{8,0},{10,2},{12,4},{14,6},{16,24},{18,... | collective-permute-start | bytes 786440 | tf_op jit(solution)/shard_map/ppermute | solution.py:82
  541.9 78.0 %collective-permute-start.97 = (bf16[128,1024]{1,0:T(8,128)(2,1)}, bf16[128,1024]{1,0:T(8,128)(2,1)S(1)}, u32[]{:S(2)}, u32[]{:S(2)}) collective-permute-start(bf16[128,1024]{1,0:T(8,128)(2,1)} %get-tuple-element.118), channel_id=1, source_target_pairs={{0,16},{2,18},{4,20},{6,22},{8,24},{10,26},{12,28},{14,30},{16,0},... | collective-permute-start | bytes 786440 | tf_op jit(solution)/shard_map/ppermute | solution.py:82
  551.9 68.5 %collective-permute-start.98 = (bf16[128,1024]{1,0:T(8,128)(2,1)}, bf16[128,1024]{1,0:T(8,128)(2,1)S(1)}, u32[]{:S(2)}, u32[]{:S(2)}) collective-permute-start(bf16[128,1024]{1,0:T(8,128)(2,1)} %get-tuple-element.117), channel_id=1, source_target_pairs={{0,24},{2,26},{4,28},{6,30},{8,16},{10,18},{12,20},{14,22},{16,8},... | collective-permute-start | bytes 786440 | tf_op jit(solution)/shard_map/ppermute | solution.py:82
  620.0 59.1 %collective-permute-start.91 = (bf16[128,2048]{1,0:T(8,128)(2,1)S(1)}, bf16[128,2048]{1,0:T(8,128)(2,1)S(1)}, u32[]{:S(2)}, u32[]{:S(2)}) collective-permute-start(bf16[128,2048]{1,0:T(8,128)(2,1)S(1)} %get-tuple-element.95), channel_id=1, source_target_pairs={{0,8},{2,10},{4,12},{6,14},{8,0},{10,2},{12,4},{14,6},{16,24},{18,... | collective-permute-start | bytes 1572872 | tf_op jit(solution)/shard_map/ppermute | solution.py:82
  620.4 60.4 %collective-permute-start.92 = (bf16[128,2048]{1,0:T(8,128)(2,1)S(1)}, bf16[128,2048]{1,0:T(8,128)(2,1)S(1)}, u32[]{:S(2)}, u32[]{:S(2)}) collective-permute-start(bf16[128,2048]{1,0:T(8,128)(2,1)S(1)} %get-tuple-element.94), channel_id=1, source_target_pairs={{0,16},{2,18},{4,20},{6,22},{8,24},{10,26},{12,28},{14,30},{16,0},... | collective-permute-start | bytes 1572872 | tf_op jit(solution)/shard_map/ppermute | solution.py:82
  626.6 64.3 %collective-permute-start.93 = (bf16[128,2048]{1,0:T(8,128)(2,1)}, bf16[128,2048]{1,0:T(8,128)(2,1)}, u32[]{:S(2)}, u32[]{:S(2)}) collective-permute-start(bf16[128,2048]{1,0:T(8,128)(2,1)} %get-tuple-element.93), channel_id=1, source_target_pairs={{0,24},{2,26},{4,28},{6,30},{8,16},{10,18},{12,20},{14,22},{16,8},... | collective-permute-start | bytes 1572872 | tf_op jit(solution)/shard_map/ppermute | solution.py:82
  629.4 70.2 %collective-permute-start.88 = (bf16[128,1024]{0,1:T(8,128)(2,1)}, bf16[128,1024]{0,1:T(8,128)(2,1)}, u32[]{:S(2)}, u32[]{:S(2)}) collective-permute-start(bf16[128,1024]{0,1:T(8,128)(2,1)} %add_convert_fusion.12), channel_id=1, source_target_pairs={{8,16},{10,18},{12,20},{14,22},{16,8},{18,10},{20,12},{22,14},{9,1... | collective-permute-start | bytes 786440 | tf_op jit(solution)/shard_map/ppermute | solution.py:82
  639.9 59.7 %collective-permute-start.86 = (bf16[128,1024]{0,1:T(8,128)(2,1)}, bf16[128,1024]{0,1:T(8,128)(2,1)}, u32[]{:S(2)}, u32[]{:S(2)}) collective-permute-start(bf16[128,1024]{0,1:T(8,128)(2,1)} %fusion.65), channel_id=1, source_target_pairs={{0,8},{2,10},{4,12},{6,14},{8,0},{10,2},{12,4},{14,6},{16,24},{18,... | collective-permute-start | bytes 786440 | tf_op jit(solution)/shard_map/ppermute | solution.py:82
  (182 other events, 3865.9 us)

commit v2 on v1

--- a/solution.py
+++ b/solution.py
@@ -143,22 +143,25 @@
         there = self.place_rows([self.over_x(part) for part in parts])
         return [here, there, self.over_core(here), self.over_core(there)]
 
-    def reduce_rows(self, left, right):
+    def reduce_rows(self, left, right, *earlier):
         width = left.shape[1]
         half, quarter = width // 2, width // 4
         away = contract_rows(left[:, half:], right).astype(bf16)
         got = self.over_core(away)
         beside = (contract_rows(left[:, quarter:half], right) + got[quarter:].astype(f32)).astype(bf16)
         beside_got = self.over_x(beside)
+        if earlier:
+            beside_got = after(beside_got, *earlier)
         here = (
             contract_rows(left[:, :quarter], right)
             + got[:quarter].astype(f32)
             + beside_got.astype(f32)
         ).astype(bf16)
         here = here.reshape(self.n, quarter // self.n, right.shape[1])
-        return [
+        parts = [
             lax.dynamic_index_in_dim(here, self.z ^ s, 0, keepdims=False) for s in range(self.n)
         ]
+        return parts, beside
 
 
 def finish_ffn(axes, both, down, gain, gate_weight, up_weight):
@@ -262,7 +265,7 @@
         ).T
 
     def gather_hidden(parts):
-        here = axes.place_rows(axes.exchange_z(parts))
+        here = axes.place_rows(parts)
         there = axes.over_x(here)
         return jnp.concatenate(
             [here, there, axes.over_core(here), axes.over_core(there)], axis=0
@@ -273,8 +276,7 @@
         for s in range(n)
     ]
     down_parts = [down_part(s) for s in range(n)]
-    both_full = gather_hidden([after(part, out_pieces[0]) for part in both_parts])
-    down_full = gather_hidden([after(part, both_full) for part in down_parts])
+    both_got = axes.exchange_z([after(part, out_pieces[0]) for part in both_parts])
 
     inputs_wide = reorder(tokens, to_block).astype(f32)
     cotangent_low = reorder(cotangent, to_block)
@@ -334,6 +336,8 @@
     probs_low = jnp.exp(scores - log_total).astype(bf16)
     attended = jnp.einsum("gmqk,kgd->qgmd", probs_low, value_head_split, preferred_element_type=f32)
     attended = attended.reshape(group_rows, heads_query * HEAD_SIZE).astype(bf16)
+    both_full = gather_hidden([after(part, attended) for part in both_got])
+    down_full = gather_hidden(axes.exchange_z([after(part, both_full) for part in down_parts]))
 
     def split_sum(pieces):
         sent = jnp.concatenate([piece(slice(own_rows, None)) for piece in pieces], axis=1)
@@ -373,19 +377,20 @@
             axes.over_y(sent[s * own_rows : (s + 1) * own_rows]) for s in range(n)
         ]
         kept = contract_cols(left[:line_rows], right)
-        return axes.scatter_z(
+        total = axes.scatter_z(
             [
                 kept[s * own_rows : (s + 1) * own_rows] + got[s].astype(f32)
                 for s in range(n)
             ]
         )
-
-    normed_two_grad = scatter_tokens(both_grad, both_full)
-    branch_feed = scatter_tokens(after(hidden, normed_two_grad), down_full)
+        return total, got[0]
+
+    normed_two_grad, _ = scatter_tokens(both_grad, both_full)
+    branch_feed, feed_got = scatter_tokens(after(hidden, normed_two_grad), down_full)
     output = reorder((resid + branch_feed).astype(bf16), to_place)
 
-    down_sums = axes.reduce_rows(cotangent_all, hidden)
-    both_sums = axes.reduce_rows(normed_two_all, both_grad)
+    down_sums, _ = axes.reduce_rows(cotangent_all, hidden)
+    both_sums, both_beside = axes.reduce_rows(normed_two_all, both_grad)
     down_got = axes.exchange_z(down_sums)
     both_got = axes.exchange_z(both_sums)
     grad_gate, grad_up, grad_down, gain_two_sum = finish_ffn(
@@ -395,7 +400,9 @@
     resid_grad = cotangent_low.astype(f32) + norm_back(resid, inverse_two, normed_two_grad)
     resid_low_all = pair_rows(resid_grad.astype(bf16))
     attended_grad = sum(dot(columns(resid_low_all, i), out_pieces[i]) for i in range(4))
-    out_sum = axes.scatter_z(axes.reduce_rows(resid_low_all, attended))
+    out_sum = axes.scatter_z(
+        axes.reduce_rows(resid_low_all, attended, both_sums[1], *down_got[1:])[0]
+    )
     attended_heads = attended_grad.astype(bf16).reshape(
         group_rows, heads_kv, group_size, HEAD_SIZE
     )
@@ -404,7 +411,7 @@
         "qgmd,kgd->gmqk", attended_heads, value_head_split, preferred_element_type=f32
     )
     row_delta = jnp.sum(prob_grad * probs_full, axis=-1, keepdims=True)
-    score_grad = (probs_full * (prob_grad - row_delta)).astype(bf16)
+    score_grad = after((probs_full * (prob_grad - row_delta)).astype(bf16), both_beside, feed_got)
     value_grad = jnp.einsum("gmqk,qgmd->kgd", probs_low, attended_heads, preferred_element_type=f32)
     value_grad = value_grad.reshape(group_rows, key_cols).astype(bf16)
     query_grad = (
@@ -428,7 +435,7 @@
     normed_one_grad = split_sum(
         [lambda rows, i=i: contract_cols(qkv_grad[rows], qkv_pieces[i]) for i in range(4)]
     )
-    qkv_sum = axes.scatter_z(axes.reduce_rows(normed_one_all, qkv_grad))
+    qkv_sum = axes.scatter_z(axes.reduce_rows(normed_one_all, qkv_grad)[0])
     token_grad = reorder(
         resid_grad + norm_back(inputs_wide, inverse_one, normed_one_grad), to_place
     )

time: 714 us -> 731 us (1.024)
  matrix products: 127 us -> 137 us
  local copies, waits for them, and re-layouts: 48.5 us -> 57.2 us
    ppermute x22, waiting for transfers between devices: 60.7 us -> 51.7 us  [over_y(): return lax.ppermute(value, 'tp', [(0, 1), (1, 0)])]
    ppermute x52, starting transfers between devices: 148 us -> 140 us  [over_z(): lax.ppermute(value, 'dp', [(a * 4 + low, b * 4 + low) for a, b in pairs f...]
    sub x0 -> x1, matrix products: none -> 7.44 us  [shards(): prob_grad - row_delta]
    unnamed x232 -> x226, local copies, waits for them, and re-layouts: 24.9 us -> 29.2 us
  transfers between devices with their start and end apart: 100 -> 100, of which waited for: 37 -> 34; matrix products, arithmetic and copies ran while one was open for 30% -> 32% of each run, Pallas kernels for 3% -> 3%
where the time goes in v2:
time: 731 us; the launch traced here: 724 us
  waiting for transfers between devices  254 us (35%)
  starting transfers between devices  184 us (25%)
  matrix products  137 us (19%)
  other arithmetic  63.6 us (9%)
  local copies, waits for them, and re-layouts  57.2 us (8%)
  Pallas kernels  23.2 us (3%)
    ppermute x52, starting transfers between devices, over_z(): lax.ppermute(value, 'dp', [(a * 4 + low, b * 4 + low) for a, b in pairs f...  140 us
    ppermute x52, waiting for transfers between devices, over_z(): lax.ppermute(value, 'dp', [(a * 4 + low, b * 4 + low) for a, b in pairs f...  131 us
    ppermute x14, waiting for transfers between devices, over_x(): return lax.ppermute(value, 'dp', [(i, i ^ 2) for i in range(self.dp)])  72 us
    ppermute x22, waiting for transfers between devices, over_y(): return lax.ppermute(value, 'tp', [(0, 1), (1, 0)])  51.7 us
    dot_general x20, matrix products, contract_cols(): lax.dot_general(left, right, (((1,), (1,)), ((), ())), preferred_element_...  47.2 us
    dot_general x12, matrix products, contract_rows(): lax.dot_general(left, right, (((0,), (0,)), ((), ())), preferred_element_...  37.3 us
    dot_general x10, matrix products, dot(): return jnp.dot(left, right, preferred_element_type=f32)  37.2 us
    unnamed x226, local copies, waits for them, and re-layouts  29.2 us
  transfers between devices with their start and end apart: 100, of which 34 were waited for; matrix products, arithmetic and copies ran while one was open for 32% of the time, Pallas kernels for 3%

profile of v2, /device:TPU:0, one launch (start us, length us, event | category | flops | bytes accessed | tf_op | source)
XLA Modules:
  0.0 723.8 jit_solution(483289616790998740)
XLA Ops:
  22.3 9.5 %collective-permute-done.3 = bf16[128,1536]{1,0:T(8,128)(2,1)S(1)} collective-permute-done((bf16[128,1536]{1,0:T(8,128)(2,1)}, bf16[128,1536]{1,0:T(8,128)(2,1)S(1)}, u32[]{:S(2)}, u32[]{:S(2)}) %collective-permute-start.3) | collective-permute-done | bytes 393248 | tf_op jit(solution)/shard_map/ppermute | solution.py:82
  59.0 10.5 %collective-permute-done.14 = bf16[128,1024]{1,0:T(8,128)(2,1)S(1)} collective-permute-done((bf16[128,1024]{1,0:T(8,128)(2,1)}, bf16[128,1024]{1,0:T(8,128)(2,1)S(1)}, u32[]{:S(2)}, u32[]{:S(2)}) %collective-permute-start.14) | collective-permute-done | bytes 262176 | tf_op jit(solution)/shard_map/ppermute | solution.py:82
  118.5 18.4 %collective-permute-done.34.refs_2_ = bf16[128,2048]{1,0:T(8,128)(2,1)} collective-permute-done((bf16[128,2048]{1,0:T(8,128)(2,1)}, bf16[128,2048]{1,0:T(8,128)(2,1)}, u32[]{:S(2)}, u32[]{:S(2)}) %collective-permute-start.34) | collective-permute-done | bytes 524320 | tf_op jit(solution)/shard_map/ppermute | solution.py:82
  159.1 11.8 %collective-permute-start.24 = (bf16[128,2048]{1,0:T(8,128)(2,1)}, bf16[128,2048]{1,0:T(8,128)(2,1)}, u32[]{:S(2)}, u32[]{:S(2)}) collective-permute-start(bf16[128,2048]{1,0:T(8,128)(2,1)} %get-tuple-element.89), channel_id=1, source_target_pairs={{0,8},{2,10},{4,12},{6,14},{8,0},{10,2},{12,4},{14,6},{16,24},{18,... | collective-permute-start | bytes 1572872 | tf_op jit(solution)/shard_map/ppermute | solution.py:82
  172.4 8.3 %collective-permute-done.24 = bf16[128,2048]{1,0:T(8,128)(2,1)} collective-permute-done((bf16[128,2048]{1,0:T(8,128)(2,1)}, bf16[128,2048]{1,0:T(8,128)(2,1)}, u32[]{:S(2)}, u32[]{:S(2)}) %collective-permute-start.24) | collective-permute-done | bytes 524320 | tf_op jit(solution)/shard_map/ppermute | solution.py:82
  189.7 12.2 %collective-permute-done.26 = bf16[128,2048]{1,0:T(8,128)(2,1)S(1)} collective-permute-done((bf16[128,2048]{1,0:T(8,128)(2,1)}, bf16[128,2048]{1,0:T(8,128)(2,1)S(1)}, u32[]{:S(2)}, u32[]{:S(2)}) %collective-permute-start.26) | collective-permute-done | bytes 524320 | tf_op jit(solution)/shard_map/ppermute | solution.py:82
  217.8 9.8 %collective-permute-done.31 = bf16[128,2048]{1,0:T(8,128)(2,1)S(1)} collective-permute-done((bf16[128,2048]{1,0:T(8,128)(2,1)S(1)}, bf16[128,2048]{1,0:T(8,128)(2,1)S(1)}, u32[]{:S(2)}, u32[]{:S(2)}) %collective-permute-start.31) | collective-permute-done | bytes 524320 | tf_op jit(solution)/shard_map/ppermute | solution.py:79
  256.5 7.0 pad_maximum_fusion
  266.5 7.8 %collective-permute-done.41 = bf16[128,2048]{1,0:T(8,128)(2,1)S(1)} collective-permute-done((bf16[128,2048]{1,0:T(8,128)(2,1)}, bf16[128,2048]{1,0:T(8,128)(2,1)S(1)}, u32[]{:S(2)}, u32[]{:S(2)}) %collective-permute-start.41) | collective-permute-done | bytes 524320 | tf_op jit(solution)/shard_map/ppermute | solution.py:82
  281.7 7.7 %collective-permute-done.49.refs_2_ = bf16[128,1024]{1,0:T(8,128)(2,1)} collective-permute-done((bf16[128,1024]{1,0:T(8,128)(2,1)S(1)}, bf16[128,1024]{1,0:T(8,128)(2,1)}, u32[]{:S(2)}, u32[]{:S(2)}) %collective-permute-start.49) | collective-permute-done | bytes 262176 | tf_op jit(solution)/shard_map/ppermute | solution.py:82
  295.1 14.4 %fusion.173 = f32[1024,2048]{1,0:T(8,128)} fusion(bf16[1024,2048]{1,0:T(8,128)(2,1)} %constant_dynamic-update-slice_fusion, bf16[2048,2048]{1,0:T(8,128)(2,1)} %pad_maximum_fusion), kind=kOutput, calls=%fused_computation.363 | convolution fusion | flops 8589934592 | bytes 20971520 | tf_op jit(solution)/shard_map/dot_general | solution.py:47
  331.9 11.5 %multiply_convert_fusion = (bf16[1024,1024]{1,0:T(8,128)(2,1)S(1)}, bf16[1024,1024]{1,0:T(8,128)(2,1)}, bf16[1024,1024]{1,0:T(8,128)(2,1)S(1)}) fusion(f32[1024,2048]{1,0:T(8,128)} %fusion.173, bf16[1024,2048]{1,0:T(8,128)(2,1)} %constant_dynamic-update-slice_fusion.8, bf16[512,1024]{1,0:T(8,128)(2,1)S(1)} %collective-permute-done.53, ...), kind=kOutput, calls=%fused_computation.19 | convolution fusion | flops 4327473152 | bytes 23068672 | tf_op jit(solution)/shard_map/dot_general | solution.py:47
  365.4 7.2 collective-permute-start.58
  427.3 8.0 %fusion.56 = f32[512,2048]{1,0:T(8,128)} fusion(bf16[1024,1024]{1,0:T(8,128)(2,1)S(1)} %get-tuple-element.47, bf16[512,1024]{1,0:T(8,128)(2,1)S(1)} %copy-done.94, bf16[512,1024]{1,0:T(8,128)(2,1)S(1)} %copy-done.92, bf16[512,1024]{1,0:T(8,128)(2,1)S(1)} %copy-done.90, bf16[512,1024]{1,0:T(8,128)(2,1)S(1)} %bitcast.329), kind=kOutput, calls=%fused_computation.136 | convolution fusion | flops 2164260864 | bytes 9437184 | tf_op jit(solution)/shard_map/dot_general | solution.py:55
  443.6 10.2 %collective-permute-done.66 = bf16[128,2048]{1,0:T(8,128)(2,1)} collective-permute-done((bf16[128,2048]{1,0:T(8,128)(2,1)}, bf16[128,2048]{1,0:T(8,128)(2,1)}, u32[]{:S(2)}, u32[]{:S(2)}) %collective-permute-start.66) | collective-permute-done | bytes 524320 | tf_op jit(solution)/shard_map/ppermute | solution.py:79
  465.3 7.4 %fusion.2 = bf16[4,4,256,256]{2,3,1,0:T(8,128)(2,1)} fusion(f32[4,256,256,4]{2,1,3,0:T(8,128)} %copy-done.23, f32[4,4,256]{2,1,0:T(4,128)S(1)} %bitcast.357, pred[256,256]{0,1:T(8,128)(4,1)S(1)} %or_and_fusion, bf16[256,4,64,1]{0,2,3,1:T(8,128)(2,1)S(1)} %bitcast.352, bf16[256,4,4,64]{0,3,2,1:T(8,128)(2,1)} %bitcast.347), kind=kOutput, calls=%fused_computation.15 | convolution fusion | flops 278925568 | bytes 7028736 | tf_op jit(solution)/shard_map/sub | solution.py:414
  485.6 7.0 collective-permute-start.70
  496.2 8.4 %collective-permute-done.70 = bf16[128,2048]{1,0:T(8,128)(2,1)S(1)} collective-permute-done((bf16[128,2048]{1,0:T(8,128)(2,1)S(1)}, bf16[128,2048]{1,0:T(8,128)(2,1)S(1)}, u32[]{:S(2)}, u32[]{:S(2)}) %collective-permute-start.70) | collective-permute-done | bytes 524320 | tf_op jit(solution)/shard_map/ppermute | solution.py:82
  532.2 23.3 %collective-permute-done.85 = bf16[512,2048]{1,0:T(8,128)(2,1)S(1)} collective-permute-done((bf16[512,2048]{1,0:T(8,128)(2,1)S(1)}, bf16[512,2048]{1,0:T(8,128)(2,1)S(1)}, u32[]{:S(2)}, u32[]{:S(2)}) %collective-permute-start.85) | collective-permute-done | bytes 2097184 | tf_op jit(solution)/shard_map/ppermute | solution.py:76
  566.3 11.7 %collective-permute-done.84 = bf16[512,1024]{1,0:T(8,128)(2,1)S(1)} collective-permute-done((bf16[512,1024]{1,0:T(8,128)(2,1)S(1)}, bf16[512,1024]{1,0:T(8,128)(2,1)S(1)}, u32[]{:S(2)}, u32[]{:S(2)}) %collective-permute-start.84) | collective-permute-done | bytes 1048608 | tf_op jit(solution)/shard_map/ppermute | solution.py:76
  586.7 22.2 %collective-permute-done.76 = bf16[512,1536]{1,0:T(8,128)(2,1)} collective-permute-done((bf16[512,1536]{1,0:T(8,128)(2,1)}, bf16[512,1536]{1,0:T(8,128)(2,1)}, u32[]{:S(2)}, u32[]{:S(2)}) %collective-permute-start.76) | collective-permute-done | bytes 1572896 | tf_op jit(solution)/shard_map/ppermute | solution.py:76
  629.6 11.1 %collective-permute-done.94 = bf16[128,1024]{0,1:T(8,128)(2,1)S(1)} collective-permute-done((bf16[128,1024]{0,1:T(8,128)(2,1)}, bf16[128,1024]{0,1:T(8,128)(2,1)S(1)}, u32[]{:S(2)}, u32[]{:S(2)}) %collective-permute-start.94) | collective-permute-done | bytes 262176 | tf_op jit(solution)/shard_map/ppermute | solution.py:82
  647.5 7.0 collective-permute-done.80
  659.3 35.1 %collective-permute-start.93 = (bf16[128,1024]{0,1:T(8,128)(2,1)}, bf16[128,1024]{0,1:T(8,128)(2,1)}, u32[]{:S(2)}, u32[]{:S(2)}) collective-permute-start(bf16[128,1024]{0,1:T(8,128)(2,1)} %fusion.69), channel_id=1, source_target_pairs={{0,8},{2,10},{4,12},{6,14},{8,0},{10,2},{12,4},{14,6},{16,24},{18,... | collective-permute-start | bytes 786440 | tf_op jit(solution)/shard_map/ppermute | solution.py:82
  (563 shorter events, 432.3 us)
Async XLA Ops:
  2.7 45.4 %collective-permute-start.6 = (bf16[128,1536]{1,0:T(8,128)(2,1)S(1)}, bf16[128,1536]{1,0:T(8,128)(2,1)}, u32[]{:S(2)}, u32[]{:S(2)}) collective-permute-start(bf16[128,1536]{1,0:T(8,128)(2,1)S(1)} %fusion.58.refs_0_), channel_id=1, source_target_pairs={{0,4},{2,6},{4,0},{6,2},{8,12},{10,14},{12,8},{14,10},{16,20},{18,... | collective-permute-start | bytes 1179656 | tf_op jit(solution)/shard_map/ppermute | solution.py:76
  46.1 55.9 %collective-permute-start.10 = (bf16[512,1536]{1,0:T(8,128)(2,1)}, bf16[512,1536]{1,0:T(8,128)(2,1)}, u32[]{:S(2)}, u32[]{:S(2)}) collective-permute-start(bf16[512,1536]{1,0:T(8,128)(2,1)} %bitcast.266), channel_id=1, source_target_pairs={{0,2},{2,0},{4,6},{6,4},{8,10},{10,8},{12,14},{14,12},{16,18},{18,... | collective-permute-start | bytes 4718600 | tf_op jit(solution)/shard_map/ppermute | solution.py:73
  54.5 51.5 %collective-permute-start.11 = (bf16[512,1536]{1,0:T(8,128)(2,1)}, bf16[512,1536]{1,0:T(8,128)(2,1)}, u32[]{:S(2)}, u32[]{:S(2)}) collective-permute-start(bf16[512,1536]{1,0:T(8,128)(2,1)} %bitcast.270), channel_id=1, source_target_pairs={{0,2},{2,0},{4,6},{6,4},{8,10},{10,8},{12,14},{14,12},{16,18},{18,... | collective-permute-start | bytes 4718600 | tf_op jit(solution)/shard_map/ppermute | solution.py:73
  89.9 53.1 %collective-permute-start.21 = (bf16[512,1024]{1,0:T(8,128)(2,1)}, bf16[512,1024]{1,0:T(8,128)(2,1)}, u32[]{:S(2)}, u32[]{:S(2)}) collective-permute-start(bf16[512,1024]{1,0:T(8,128)(2,1)} %bitcast.274), channel_id=1, source_target_pairs={{0,2},{2,0},{4,6},{6,4},{8,10},{10,8},{12,14},{14,12},{16,18},{18,... | collective-permute-start | bytes 3145736 | tf_op jit(solution)/shard_map/ppermute | solution.py:73
  140.7 64.8 %collective-permute-start.36 = (bf16[512,2048]{1,0:T(8,128)(2,1)}, bf16[512,2048]{1,0:T(8,128)(2,1)}, u32[]{:S(2)}, u32[]{:S(2)}) collective-permute-start(bf16[512,2048]{1,0:T(8,128)(2,1)} %bitcast.289), channel_id=1, source_target_pairs={{0,4},{2,6},{4,0},{6,2},{8,12},{10,14},{12,8},{14,10},{16,20},{18,... | collective-permute-start | bytes 6291464 | tf_op jit(solution)/shard_map/ppermute | solution.py:76
  184.8 69.8 %collective-permute-start.37 = (bf16[512,2048]{1,0:T(8,128)(2,1)}, bf16[512,2048]{1,0:T(8,128)(2,1)}, u32[]{:S(2)}, u32[]{:S(2)}) collective-permute-start(bf16[512,2048]{1,0:T(8,128)(2,1)} %bitcast.290), channel_id=1, source_target_pairs={{0,2},{2,0},{4,6},{6,4},{8,10},{10,8},{12,14},{14,12},{16,18},{18,... | collective-permute-start | bytes 6291464 | tf_op jit(solution)/shard_map/ppermute | solution.py:73
  209.8 46.7 %collective-permute-start.38 = (bf16[512,2048]{1,0:T(8,128)(2,1)}, bf16[512,2048]{1,0:T(8,128)(2,1)}, u32[]{:S(2)}, u32[]{:S(2)}) collective-permute-start(bf16[512,2048]{1,0:T(8,128)(2,1)} %collective-permute-done.36), channel_id=1, source_target_pairs={{0,2},{2,0},{4,6},{6,4},{8,10},{10,8},{12,14},{14,12},{16,18},{18,... | collective-permute-start | bytes 6291464 | tf_op jit(solution)/shard_map/ppermute | solution.py:73
  248.9 67.7 %collective-permute-start.44 = (bf16[128,2048]{1,0:T(8,128)(2,1)S(1)}, bf16[128,2048]{1,0:T(8,128)(2,1)}, u32[]{:S(2)}, u32[]{:S(2)}) collective-permute-start(bf16[128,2048]{1,0:T(8,128)(2,1)S(1)} %copy_bitcast_fusion.1), channel_id=1, source_target_pairs={{0,1},{1,0},{2,3},{3,2},{4,5},{5,4},{6,7},{7,6},{8,9},{9,8},{10,11... | collective-permute-start | bytes 1572872 | tf_op jit(solution)/shard_map/ppermute | solution.py:79
  254.6 66.1 %collective-permute-start.45 = (bf16[128,2048]{1,0:T(8,128)(2,1)}, bf16[128,2048]{1,0:T(8,128)(2,1)}, u32[]{:S(2)}, u32[]{:S(2)}) collective-permute-start(bf16[128,2048]{1,0:T(8,128)(2,1)} %collective-permute-done.39), channel_id=1, source_target_pairs={{0,1},{1,0},{2,3},{3,2},{4,5},{5,4},{6,7},{7,6},{8,9},{9,8},{10,11... | collective-permute-start | bytes 1572872 | tf_op jit(solution)/shard_map/ppermute | solution.py:79
  407.4 72.9 %collective-permute-start.73 = (bf16[1024,2048]{1,0:T(8,128)(2,1)}, bf16[1024,2048]{1,0:T(8,128)(2,1)}, u32[]{:S(2)}, u32[]{:S(2)}) collective-permute-start(bf16[1024,2048]{1,0:T(8,128)(2,1)} %convolution_convert_fusion.1), channel_id=1, source_target_pairs={{0,2},{2,0},{4,6},{6,4},{8,10},{10,8},{12,14},{14,12},{16,18},{18,... | collective-permute-start | bytes 12582920 | tf_op jit(solution)/shard_map/ppermute | solution.py:73
  411.7 62.8 %collective-permute-start.87 = (bf16[512,1024]{1,0:T(8,128)(2,1)}, bf16[512,1024]{1,0:T(8,128)(2,1)}, u32[]{:S(2)}, u32[]{:S(2)}) collective-permute-start(bf16[512,1024]{1,0:T(8,128)(2,1)} %add_convert_fusion.4), channel_id=1, source_target_pairs={{0,4},{2,6},{4,0},{6,2},{8,12},{10,14},{12,8},{14,10},{16,20},{18,... | collective-permute-start | bytes 3145736 | tf_op jit(solution)/shard_map/ppermute | solution.py:76
  425.2 60.3 %collective-permute-start.63 = (bf16[128,2048]{1,0:T(8,128)(2,1)}, bf16[128,2048]{1,0:T(8,128)(2,1)}, u32[]{:S(2)}, u32[]{:S(2)}) collective-permute-start(bf16[128,2048]{1,0:T(8,128)(2,1)} %get-tuple-element.109), channel_id=1, source_target_pairs={{0,1},{1,0},{2,3},{3,2},{4,5},{5,4},{6,7},{7,6},{8,9},{9,8},{10,11... | collective-permute-start | bytes 1572872 | tf_op jit(solution)/shard_map/ppermute | solution.py:79
  478.7 82.4 %collective-permute-start.88 = (bf16[128,1024]{1,0:T(8,128)(2,1)S(1)}, bf16[128,1024]{1,0:T(8,128)(2,1)S(1)}, u32[]{:S(2)}, u32[]{:S(2)}) collective-permute-start(bf16[128,1024]{1,0:T(8,128)(2,1)S(1)} %get-tuple-element.132), channel_id=1, source_target_pairs={{0,8},{2,10},{4,12},{6,14},{8,0},{10,2},{12,4},{14,6},{16,24},{18,... | collective-permute-start | bytes 786440 | tf_op jit(solution)/shard_map/ppermute | solution.py:82
  496.0 66.8 %collective-permute-start.89 = (bf16[128,1024]{1,0:T(8,128)(2,1)S(1)}, bf16[128,1024]{1,0:T(8,128)(2,1)S(1)}, u32[]{:S(2)}, u32[]{:S(2)}) collective-permute-start(bf16[128,1024]{1,0:T(8,128)(2,1)S(1)} %get-tuple-element.131), channel_id=1, source_target_pairs={{0,16},{2,18},{4,20},{6,22},{8,24},{10,26},{12,28},{14,30},{16,0},... | collective-permute-start | bytes 786440 | tf_op jit(solution)/shard_map/ppermute | solution.py:82
  507.1 48.5 %collective-permute-start.85 = (bf16[512,2048]{1,0:T(8,128)(2,1)S(1)}, bf16[512,2048]{1,0:T(8,128)(2,1)S(1)}, u32[]{:S(2)}, u32[]{:S(2)}) collective-permute-start(bf16[512,2048]{1,0:T(8,128)(2,1)S(1)} %add_convert_fusion.1), channel_id=1, source_target_pairs={{0,4},{2,6},{4,0},{6,2},{8,12},{10,14},{12,8},{14,10},{16,20},{18,... | collective-permute-start | bytes 6291464 | tf_op jit(solution)/shard_map/ppermute | solution.py:76
  520.6 57.4 %collective-permute-start.84 = (bf16[512,1024]{1,0:T(8,128)(2,1)S(1)}, bf16[512,1024]{1,0:T(8,128)(2,1)S(1)}, u32[]{:S(2)}, u32[]{:S(2)}) collective-permute-start(bf16[512,1024]{1,0:T(8,128)(2,1)S(1)} %add_convert_fusion.5), channel_id=1, source_target_pairs={{0,4},{2,6},{4,0},{6,2},{8,12},{10,14},{12,8},{14,10},{16,20},{18,... | collective-permute-start | bytes 3145736 | tf_op jit(solution)/shard_map/ppermute | solution.py:76
  530.3 78.6 %collective-permute-start.76 = (bf16[512,1536]{1,0:T(8,128)(2,1)}, bf16[512,1536]{1,0:T(8,128)(2,1)}, u32[]{:S(2)}, u32[]{:S(2)}) collective-permute-start(bf16[512,1536]{1,0:T(8,128)(2,1)} %fusion.6), channel_id=1, source_target_pairs={{0,4},{2,6},{4,0},{6,2},{8,12},{10,14},{12,8},{14,10},{16,20},{18,... | collective-permute-start | bytes 4718600 | tf_op jit(solution)/shard_map/ppermute | solution.py:76
  561.2 97.1 %collective-permute-start.71 = (bf16[128,2048]{1,0:T(8,128)(2,1)}, bf16[128,2048]{1,0:T(8,128)(2,1)}, u32[]{:S(2)}, u32[]{:S(2)}) collective-permute-start(bf16[128,2048]{1,0:T(8,128)(2,1)} %get-tuple-element.100), channel_id=1, source_target_pairs={{8,16},{10,18},{12,20},{14,22},{16,8},{18,10},{20,12},{22,14},{9,1... | collective-permute-start | bytes 1572872 | tf_op jit(solution)/shard_map/ppermute | solution.py:82
  562.8 96.5 %collective-permute-start.69 = (bf16[128,2048]{1,0:T(8,128)(2,1)}, bf16[128,2048]{1,0:T(8,128)(2,1)}, u32[]{:S(2)}, u32[]{:S(2)}) collective-permute-start(bf16[128,2048]{1,0:T(8,128)(2,1)} %get-tuple-element.99), channel_id=1, source_target_pairs={{0,8},{2,10},{4,12},{6,14},{8,0},{10,2},{12,4},{14,6},{16,24},{18,... | collective-permute-start | bytes 1572872 | tf_op jit(solution)/shard_map/ppermute | solution.py:82
  618.7 75.7 %collective-permute-start.96 = (bf16[128,2048]{1,0:T(8,128)(2,1)}, bf16[128,2048]{1,0:T(8,128)(2,1)}, u32[]{:S(2)}, u32[]{:S(2)}) collective-permute-start(bf16[128,2048]{1,0:T(8,128)(2,1)} %get-tuple-element.108), channel_id=1, source_target_pairs={{0,8},{2,10},{4,12},{6,14},{8,0},{10,2},{12,4},{14,6},{16,24},{18,... | collective-permute-start | bytes 1572872 | tf_op jit(solution)/shard_map/ppermute | solution.py:82
  646.7 49.0 %collective-permute-start.97 = (bf16[128,2048]{1,0:T(8,128)(2,1)}, bf16[128,2048]{1,0:T(8,128)(2,1)S(1)}, u32[]{:S(2)}, u32[]{:S(2)}) collective-permute-start(bf16[128,2048]{1,0:T(8,128)(2,1)} %get-tuple-element.106), channel_id=1, source_target_pairs={{0,16},{2,18},{4,20},{6,22},{8,24},{10,26},{12,28},{14,30},{16,0},... | collective-permute-start | bytes 1572872 | tf_op jit(solution)/shard_map/ppermute | solution.py:82
  656.1 47.7 %collective-permute-start.98 = (bf16[128,2048]{1,0:T(8,128)(2,1)}, bf16[128,2048]{1,0:T(8,128)(2,1)}, u32[]{:S(2)}, u32[]{:S(2)}) collective-permute-start(bf16[128,2048]{1,0:T(8,128)(2,1)} %get-tuple-element.105), channel_id=1, source_target_pairs={{0,24},{2,26},{4,28},{6,30},{8,16},{10,18},{12,20},{14,22},{16,8},... | collective-permute-start | bytes 1572872 | tf_op jit(solution)/shard_map/ppermute | solution.py:82
  658.3 57.4 %collective-permute-start.95 = (bf16[128,1024]{0,1:T(8,128)(2,1)}, bf16[128,1024]{0,1:T(8,128)(2,1)S(1)}, u32[]{:S(2)}, u32[]{:S(2)}) collective-permute-start(bf16[128,1024]{0,1:T(8,128)(2,1)} %add_convert_fusion.12), channel_id=1, source_target_pairs={{8,16},{10,18},{12,20},{14,22},{16,8},{18,10},{20,12},{22,14},{9,1... | collective-permute-start | bytes 786440 | tf_op jit(solution)/shard_map/ppermute | solution.py:82
  659.3 56.4 %collective-permute-start.93 = (bf16[128,1024]{0,1:T(8,128)(2,1)}, bf16[128,1024]{0,1:T(8,128)(2,1)}, u32[]{:S(2)}, u32[]{:S(2)}) collective-permute-start(bf16[128,1024]{0,1:T(8,128)(2,1)} %fusion.69), channel_id=1, source_target_pairs={{0,8},{2,10},{4,12},{6,14},{8,0},{10,2},{12,4},{14,6},{16,24},{18,... | collective-permute-start | bytes 786440 | tf_op jit(solution)/shard_map/ppermute | solution.py:82
  (179 other events, 4330.5 us)

commit v3 on v2

--- a/solution.py
+++ b/solution.py
@@ -401,7 +401,7 @@
     resid_low_all = pair_rows(resid_grad.astype(bf16))
     attended_grad = sum(dot(columns(resid_low_all, i), out_pieces[i]) for i in range(4))
     out_sum = axes.scatter_z(
-        axes.reduce_rows(resid_low_all, attended, both_sums[1], *down_got[1:])[0]
+        axes.reduce_rows(resid_low_all, attended, both_sums[1])[0]
     )
     attended_heads = attended_grad.astype(bf16).reshape(
         group_rows, heads_kv, group_size, HEAD_SIZE

time: 731 us -> 737 us (level)
    unnamed x226 -> x222, local copies, waits for them, and re-layouts: 29.2 us -> 29.2 us
where the time goes in v3:
time: 737 us; the launch traced here: 731 us
  waiting for transfers between devices  256 us (35%)
  starting transfers between devices  190 us (26%)
  matrix products  137 us (19%)
  other arithmetic  63.3 us (9%)
  local copies, waits for them, and re-layouts  57.5 us (8%)
  Pallas kernels  23.2 us (3%)
    ppermute x52, starting transfers between devices, over_z(): lax.ppermute(value, 'dp', [(a * 4 + low, b * 4 + low) for a, b in pairs f...  146 us
    ppermute x52, waiting for transfers between devices, over_z(): lax.ppermute(value, 'dp', [(a * 4 + low, b * 4 + low) for a, b in pairs f...  127 us
    ppermute x14, waiting for transfers between devices, over_x(): return lax.ppermute(value, 'dp', [(i, i ^ 2) for i in range(self.dp)])  77.2 us
    ppermute x22, waiting for transfers between devices, over_y(): return lax.ppermute(value, 'tp', [(0, 1), (1, 0)])  51.5 us
    dot_general x20, matrix products, contract_cols(): lax.dot_general(left, right, (((1,), (1,)), ((), ())), preferred_element_...  47.2 us
    dot_general x12, matrix products, contract_rows(): lax.dot_general(left, right, (((0,), (0,)), ((), ())), preferred_element_...  37.3 us
    dot_general x10, matrix products, dot(): return jnp.dot(left, right, preferred_element_type=f32)  37.3 us
    unnamed x222, local copies, waits for them, and re-layouts  29.2 us
  transfers between devices with their start and end apart: 100, of which 34 were waited for; matrix products, arithmetic and copies ran while one was open for 32% of the time, Pallas kernels for 3%

profile of v3, /device:TPU:0, one launch (start us, length us, event | category | flops | bytes accessed | tf_op | source)
XLA Modules:
  0.0 730.7 jit_solution(15216516580312386905)
XLA Ops:
  22.4 9.5 %collective-permute-done.3 = bf16[128,1536]{1,0:T(8,128)(2,1)S(1)} collective-permute-done((bf16[128,1536]{1,0:T(8,128)(2,1)}, bf16[128,1536]{1,0:T(8,128)(2,1)S(1)}, u32[]{:S(2)}, u32[]{:S(2)}) %collective-permute-start.3) | collective-permute-done | bytes 393248 | tf_op jit(solution)/shard_map/ppermute | solution.py:82
  59.0 10.6 %collective-permute-done.14 = bf16[128,1024]{1,0:T(8,128)(2,1)S(1)} collective-permute-done((bf16[128,1024]{1,0:T(8,128)(2,1)}, bf16[128,1024]{1,0:T(8,128)(2,1)S(1)}, u32[]{:S(2)}, u32[]{:S(2)}) %collective-permute-start.14) | collective-permute-done | bytes 262176 | tf_op jit(solution)/shard_map/ppermute | solution.py:82
  118.6 18.4 %collective-permute-done.34.refs_2_ = bf16[128,2048]{1,0:T(8,128)(2,1)} collective-permute-done((bf16[128,2048]{1,0:T(8,128)(2,1)}, bf16[128,2048]{1,0:T(8,128)(2,1)}, u32[]{:S(2)}, u32[]{:S(2)}) %collective-permute-start.34) | collective-permute-done | bytes 524320 | tf_op jit(solution)/shard_map/ppermute | solution.py:82
  159.2 11.8 %collective-permute-start.24 = (bf16[128,2048]{1,0:T(8,128)(2,1)}, bf16[128,2048]{1,0:T(8,128)(2,1)}, u32[]{:S(2)}, u32[]{:S(2)}) collective-permute-start(bf16[128,2048]{1,0:T(8,128)(2,1)} %get-tuple-element.89), channel_id=1, source_target_pairs={{0,8},{2,10},{4,12},{6,14},{8,0},{10,2},{12,4},{14,6},{16,24},{18,... | collective-permute-start | bytes 1572872 | tf_op jit(solution)/shard_map/ppermute | solution.py:82
  172.5 8.3 %collective-permute-done.24 = bf16[128,2048]{1,0:T(8,128)(2,1)} collective-permute-done((bf16[128,2048]{1,0:T(8,128)(2,1)}, bf16[128,2048]{1,0:T(8,128)(2,1)}, u32[]{:S(2)}, u32[]{:S(2)}) %collective-permute-start.24) | collective-permute-done | bytes 524320 | tf_op jit(solution)/shard_map/ppermute | solution.py:82
  189.8 12.2 %collective-permute-done.26 = bf16[128,2048]{1,0:T(8,128)(2,1)S(1)} collective-permute-done((bf16[128,2048]{1,0:T(8,128)(2,1)}, bf16[128,2048]{1,0:T(8,128)(2,1)S(1)}, u32[]{:S(2)}, u32[]{:S(2)}) %collective-permute-start.26) | collective-permute-done | bytes 524320 | tf_op jit(solution)/shard_map/ppermute | solution.py:82
  217.9 9.7 %collective-permute-done.31 = bf16[128,2048]{1,0:T(8,128)(2,1)S(1)} collective-permute-done((bf16[128,2048]{1,0:T(8,128)(2,1)S(1)}, bf16[128,2048]{1,0:T(8,128)(2,1)S(1)}, u32[]{:S(2)}, u32[]{:S(2)}) %collective-permute-start.31) | collective-permute-done | bytes 524320 | tf_op jit(solution)/shard_map/ppermute | solution.py:79
  256.5 7.0 pad_maximum_fusion
  266.5 7.8 %collective-permute-done.41 = bf16[128,2048]{1,0:T(8,128)(2,1)S(1)} collective-permute-done((bf16[128,2048]{1,0:T(8,128)(2,1)}, bf16[128,2048]{1,0:T(8,128)(2,1)S(1)}, u32[]{:S(2)}, u32[]{:S(2)}) %collective-permute-start.41) | collective-permute-done | bytes 524320 | tf_op jit(solution)/shard_map/ppermute | solution.py:82
  281.7 7.7 %collective-permute-done.49.refs_2_ = bf16[128,1024]{1,0:T(8,128)(2,1)} collective-permute-done((bf16[128,1024]{1,0:T(8,128)(2,1)S(1)}, bf16[128,1024]{1,0:T(8,128)(2,1)}, u32[]{:S(2)}, u32[]{:S(2)}) %collective-permute-start.49) | collective-permute-done | bytes 262176 | tf_op jit(solution)/shard_map/ppermute | solution.py:82
  295.2 14.4 %fusion.173 = f32[1024,2048]{1,0:T(8,128)} fusion(bf16[1024,2048]{1,0:T(8,128)(2,1)} %constant_dynamic-update-slice_fusion, bf16[2048,2048]{1,0:T(8,128)(2,1)} %pad_maximum_fusion), kind=kOutput, calls=%fused_computation.363 | convolution fusion | flops 8589934592 | bytes 20971520 | tf_op jit(solution)/shard_map/dot_general | solution.py:47
  332.0 11.5 %multiply_convert_fusion = (bf16[1024,1024]{1,0:T(8,128)(2,1)S(1)}, bf16[1024,1024]{1,0:T(8,128)(2,1)}, bf16[1024,1024]{1,0:T(8,128)(2,1)S(1)}) fusion(f32[1024,2048]{1,0:T(8,128)} %fusion.173, bf16[1024,2048]{1,0:T(8,128)(2,1)} %constant_dynamic-update-slice_fusion.8, bf16[512,1024]{1,0:T(8,128)(2,1)S(1)} %collective-permute-done.53, ...), kind=kOutput, calls=%fused_computation.19 | convolution fusion | flops 4327473152 | bytes 23068672 | tf_op jit(solution)/shard_map/dot_general | solution.py:47
  343.5 6.7 convolution_convert_fusion.3
  365.5 7.2 collective-permute-start.58
  427.3 8.0 %fusion.56 = f32[512,2048]{1,0:T(8,128)} fusion(bf16[1024,1024]{1,0:T(8,128)(2,1)S(1)} %get-tuple-element.47, bf16[512,1024]{1,0:T(8,128)(2,1)S(1)} %copy-done.92, bf16[512,1024]{1,0:T(8,128)(2,1)S(1)} %copy-done.90, bf16[512,1024]{1,0:T(8,128)(2,1)S(1)} %copy-done.88, bf16[512,1024]{1,0:T(8,128)(2,1)S(1)} %bitcast.329), kind=kOutput, calls=%fused_computation.136 | convolution fusion | flops 2164260864 | bytes 9437184 | tf_op jit(solution)/shard_map/dot_general | solution.py:55
  443.6 10.2 %collective-permute-done.66 = bf16[128,2048]{1,0:T(8,128)(2,1)} collective-permute-done((bf16[128,2048]{1,0:T(8,128)(2,1)}, bf16[128,2048]{1,0:T(8,128)(2,1)}, u32[]{:S(2)}, u32[]{:S(2)}) %collective-permute-start.66) | collective-permute-done | bytes 524320 | tf_op jit(solution)/shard_map/ppermute | solution.py:79
  465.4 7.5 %fusion.2 = bf16[4,4,256,256]{2,3,1,0:T(8,128)(2,1)} fusion(f32[4,256,256,4]{2,1,3,0:T(8,128)} %copy-done.23, f32[4,4,256]{2,1,0:T(4,128)S(1)} %bitcast.357, pred[256,256]{0,1:T(8,128)(4,1)S(1)} %or_and_fusion, bf16[256,4,64,1]{0,2,3,1:T(8,128)(2,1)S(1)} %bitcast.352, bf16[256,4,4,64]{0,3,2,1:T(8,128)(2,1)} %bitcast.347), kind=kOutput, calls=%fused_computation.15 | convolution fusion | flops 278925568 | bytes 7028736 | tf_op jit(solution)/shard_map/sub | solution.py:414
  486.0 7.0 collective-permute-start.70
  496.6 8.4 %collective-permute-done.70 = bf16[128,2048]{1,0:T(8,128)(2,1)S(1)} collective-permute-done((bf16[128,2048]{1,0:T(8,128)(2,1)S(1)}, bf16[128,2048]{1,0:T(8,128)(2,1)S(1)}, u32[]{:S(2)}, u32[]{:S(2)}) %collective-permute-start.70) | collective-permute-done | bytes 524320 | tf_op jit(solution)/shard_map/ppermute | solution.py:82
  532.6 23.4 %collective-permute-done.85 = bf16[512,2048]{1,0:T(8,128)(2,1)S(1)} collective-permute-done((bf16[512,2048]{1,0:T(8,128)(2,1)S(1)}, bf16[512,2048]{1,0:T(8,128)(2,1)S(1)}, u32[]{:S(2)}, u32[]{:S(2)}) %collective-permute-start.85) | collective-permute-done | bytes 2097184 | tf_op jit(solution)/shard_map/ppermute | solution.py:76
  561.6 16.9 %collective-permute-done.84 = bf16[512,1024]{1,0:T(8,128)(2,1)S(1)} collective-permute-done((bf16[512,1024]{1,0:T(8,128)(2,1)S(1)}, bf16[512,1024]{1,0:T(8,128)(2,1)S(1)}, u32[]{:S(2)}, u32[]{:S(2)}) %collective-permute-start.84) | collective-permute-done | bytes 1048608 | tf_op jit(solution)/shard_map/ppermute | solution.py:76
  587.0 22.2 %collective-permute-done.76 = bf16[512,1536]{1,0:T(8,128)(2,1)} collective-permute-done((bf16[512,1536]{1,0:T(8,128)(2,1)}, bf16[512,1536]{1,0:T(8,128)(2,1)}, u32[]{:S(2)}, u32[]{:S(2)}) %collective-permute-start.76) | collective-permute-done | bytes 1572896 | tf_op jit(solution)/shard_map/ppermute | solution.py:76
  650.2 12.0 %collective-permute-done.69 = bf16[128,2048]{1,0:T(8,128)(2,1)S(1)} collective-permute-done((bf16[128,2048]{1,0:T(8,128)(2,1)}, bf16[128,2048]{1,0:T(8,128)(2,1)S(1)}, u32[]{:S(2)}, u32[]{:S(2)}) %collective-permute-start.69) | collective-permute-done | bytes 524320 | tf_op jit(solution)/shard_map/ppermute | solution.py:82
  662.3 39.1 %collective-permute-start.88 = (bf16[128,1024]{0,1:T(8,128)(2,1)}, bf16[128,1024]{0,1:T(8,128)(2,1)}, u32[]{:S(2)}, u32[]{:S(2)}) collective-permute-start(bf16[128,1024]{0,1:T(8,128)(2,1)} %fusion.69), channel_id=1, source_target_pairs={{0,8},{2,10},{4,12},{6,14},{8,0},{10,2},{12,4},{14,6},{16,24},{18,... | collective-permute-start | bytes 786440 | tf_op jit(solution)/shard_map/ppermute | solution.py:82
  (559 shorter events, 429.2 us)
Async XLA Ops:
  2.7 45.4 %collective-permute-start.6 = (bf16[128,1536]{1,0:T(8,128)(2,1)S(1)}, bf16[128,1536]{1,0:T(8,128)(2,1)}, u32[]{:S(2)}, u32[]{:S(2)}) collective-permute-start(bf16[128,1536]{1,0:T(8,128)(2,1)S(1)} %fusion.58.refs_0_), channel_id=1, source_target_pairs={{0,4},{2,6},{4,0},{6,2},{8,12},{10,14},{12,8},{14,10},{16,20},{18,... | collective-permute-start | bytes 1179656 | tf_op jit(solution)/shard_map/ppermute | solution.py:76
  46.1 55.9 %collective-permute-start.10 = (bf16[512,1536]{1,0:T(8,128)(2,1)}, bf16[512,1536]{1,0:T(8,128)(2,1)}, u32[]{:S(2)}, u32[]{:S(2)}) collective-permute-start(bf16[512,1536]{1,0:T(8,128)(2,1)} %bitcast.266), channel_id=1, source_target_pairs={{0,2},{2,0},{4,6},{6,4},{8,10},{10,8},{12,14},{14,12},{16,18},{18,... | collective-permute-start | bytes 4718600 | tf_op jit(solution)/shard_map/ppermute | solution.py:73
  54.5 51.6 %collective-permute-start.11 = (bf16[512,1536]{1,0:T(8,128)(2,1)}, bf16[512,1536]{1,0:T(8,128)(2,1)}, u32[]{:S(2)}, u32[]{:S(2)}) collective-permute-start(bf16[512,1536]{1,0:T(8,128)(2,1)} %bitcast.270), channel_id=1, source_target_pairs={{0,2},{2,0},{4,6},{6,4},{8,10},{10,8},{12,14},{14,12},{16,18},{18,... | collective-permute-start | bytes 4718600 | tf_op jit(solution)/shard_map/ppermute | solution.py:73
  90.0 53.1 %collective-permute-start.21 = (bf16[512,1024]{1,0:T(8,128)(2,1)}, bf16[512,1024]{1,0:T(8,128)(2,1)}, u32[]{:S(2)}, u32[]{:S(2)}) collective-permute-start(bf16[512,1024]{1,0:T(8,128)(2,1)} %bitcast.274), channel_id=1, source_target_pairs={{0,2},{2,0},{4,6},{6,4},{8,10},{10,8},{12,14},{14,12},{16,18},{18,... | collective-permute-start | bytes 3145736 | tf_op jit(solution)/shard_map/ppermute | solution.py:73
  140.8 64.8 %collective-permute-start.36 = (bf16[512,2048]{1,0:T(8,128)(2,1)}, bf16[512,2048]{1,0:T(8,128)(2,1)}, u32[]{:S(2)}, u32[]{:S(2)}) collective-permute-start(bf16[512,2048]{1,0:T(8,128)(2,1)} %bitcast.289), channel_id=1, source_target_pairs={{0,4},{2,6},{4,0},{6,2},{8,12},{10,14},{12,8},{14,10},{16,20},{18,... | collective-permute-start | bytes 6291464 | tf_op jit(solution)/shard_map/ppermute | solution.py:76
  184.9 69.7 %collective-permute-start.37 = (bf16[512,2048]{1,0:T(8,128)(2,1)}, bf16[512,2048]{1,0:T(8,128)(2,1)}, u32[]{:S(2)}, u32[]{:S(2)}) collective-permute-start(bf16[512,2048]{1,0:T(8,128)(2,1)} %bitcast.290), channel_id=1, source_target_pairs={{0,2},{2,0},{4,6},{6,4},{8,10},{10,8},{12,14},{14,12},{16,18},{18,... | collective-permute-start | bytes 6291464 | tf_op jit(solution)/shard_map/ppermute | solution.py:73
  209.8 46.7 %collective-permute-start.38 = (bf16[512,2048]{1,0:T(8,128)(2,1)}, bf16[512,2048]{1,0:T(8,128)(2,1)}, u32[]{:S(2)}, u32[]{:S(2)}) collective-permute-start(bf16[512,2048]{1,0:T(8,128)(2,1)} %collective-permute-done.36), channel_id=1, source_target_pairs={{0,2},{2,0},{4,6},{6,4},{8,10},{10,8},{12,14},{14,12},{16,18},{18,... | collective-permute-start | bytes 6291464 | tf_op jit(solution)/shard_map/ppermute | solution.py:73
  249.0 67.7 %collective-permute-start.44 = (bf16[128,2048]{1,0:T(8,128)(2,1)S(1)}, bf16[128,2048]{1,0:T(8,128)(2,1)}, u32[]{:S(2)}, u32[]{:S(2)}) collective-permute-start(bf16[128,2048]{1,0:T(8,128)(2,1)S(1)} %copy_bitcast_fusion.1), channel_id=1, source_target_pairs={{0,1},{1,0},{2,3},{3,2},{4,5},{5,4},{6,7},{7,6},{8,9},{9,8},{10,11... | collective-permute-start | bytes 1572872 | tf_op jit(solution)/shard_map/ppermute | solution.py:79
  254.6 66.1 %collective-permute-start.45 = (bf16[128,2048]{1,0:T(8,128)(2,1)}, bf16[128,2048]{1,0:T(8,128)(2,1)}, u32[]{:S(2)}, u32[]{:S(2)}) collective-permute-start(bf16[128,2048]{1,0:T(8,128)(2,1)} %collective-permute-done.39), channel_id=1, source_target_pairs={{0,1},{1,0},{2,3},{3,2},{4,5},{5,4},{6,7},{7,6},{8,9},{9,8},{10,11... | collective-permute-start | bytes 1572872 | tf_op jit(solution)/shard_map/ppermute | solution.py:79
  407.5 73.2 %collective-permute-start.73 = (bf16[1024,2048]{1,0:T(8,128)(2,1)}, bf16[1024,2048]{1,0:T(8,128)(2,1)}, u32[]{:S(2)}, u32[]{:S(2)}) collective-permute-start(bf16[1024,2048]{1,0:T(8,128)(2,1)} %convolution_convert_fusion.1), channel_id=1, source_target_pairs={{0,2},{2,0},{4,6},{6,4},{8,10},{10,8},{12,14},{14,12},{16,18},{18,... | collective-permute-start | bytes 12582920 | tf_op jit(solution)/shard_map/ppermute | solution.py:73
  411.7 62.8 %collective-permute-start.95 = (bf16[512,1024]{1,0:T(8,128)(2,1)}, bf16[512,1024]{1,0:T(8,128)(2,1)}, u32[]{:S(2)}, u32[]{:S(2)}) collective-permute-start(bf16[512,1024]{1,0:T(8,128)(2,1)} %add_convert_fusion.3), channel_id=1, source_target_pairs={{0,4},{2,6},{4,0},{6,2},{8,12},{10,14},{12,8},{14,10},{16,20},{18,... | collective-permute-start | bytes 3145736 | tf_op jit(solution)/shard_map/ppermute | solution.py:76
  425.3 60.6 %collective-permute-start.63 = (bf16[128,2048]{1,0:T(8,128)(2,1)}, bf16[128,2048]{1,0:T(8,128)(2,1)}, u32[]{:S(2)}, u32[]{:S(2)}) collective-permute-start(bf16[128,2048]{1,0:T(8,128)(2,1)} %get-tuple-element.109), channel_id=1, source_target_pairs={{0,1},{1,0},{2,3},{3,2},{4,5},{5,4},{6,7},{7,6},{8,9},{9,8},{10,11... | collective-permute-start | bytes 1572872 | tf_op jit(solution)/shard_map/ppermute | solution.py:79
  435.3 43.8 %collective-permute-start.65 = (bf16[128,2048]{1,0:T(8,128)(2,1)}, bf16[128,2048]{1,0:T(8,128)(2,1)}, u32[]{:S(2)}, u32[]{:S(2)}) collective-permute-start(bf16[128,2048]{1,0:T(8,128)(2,1)} %get-tuple-element.111), channel_id=1, source_target_pairs={{0,1},{1,0},{2,3},{3,2},{4,5},{5,4},{6,7},{7,6},{8,9},{9,8},{10,11... | collective-permute-start | bytes 1572872 | tf_op jit(solution)/shard_map/ppermute | solution.py:79
  479.1 159.2 %collective-permute-start.96 = (bf16[128,1024]{1,0:T(8,128)(2,1)}, bf16[128,1024]{1,0:T(8,128)(2,1)}, u32[]{:S(2)}, u32[]{:S(2)}) collective-permute-start(bf16[128,1024]{1,0:T(8,128)(2,1)} %get-tuple-element.131), channel_id=1, source_target_pairs={{0,8},{2,10},{4,12},{6,14},{8,0},{10,2},{12,4},{14,6},{16,24},{18,... | collective-permute-start | bytes 786440 | tf_op jit(solution)/shard_map/ppermute | solution.py:82
  496.4 145.5 %collective-permute-start.97 = (bf16[128,1024]{1,0:T(8,128)(2,1)}, bf16[128,1024]{1,0:T(8,128)(2,1)}, u32[]{:S(2)}, u32[]{:S(2)}) collective-permute-start(bf16[128,1024]{1,0:T(8,128)(2,1)} %get-tuple-element.130), channel_id=1, source_target_pairs={{0,16},{2,18},{4,20},{6,22},{8,24},{10,26},{12,28},{14,30},{16,0},... | collective-permute-start | bytes 786440 | tf_op jit(solution)/shard_map/ppermute | solution.py:82
  507.5 48.5 %collective-permute-start.85 = (bf16[512,2048]{1,0:T(8,128)(2,1)S(1)}, bf16[512,2048]{1,0:T(8,128)(2,1)S(1)}, u32[]{:S(2)}, u32[]{:S(2)}) collective-permute-start(bf16[512,2048]{1,0:T(8,128)(2,1)S(1)} %add_convert_fusion.1), channel_id=1, source_target_pairs={{0,4},{2,6},{4,0},{6,2},{8,12},{10,14},{12,8},{14,10},{16,20},{18,... | collective-permute-start | bytes 6291464 | tf_op jit(solution)/shard_map/ppermute | solution.py:76
  521.0 57.5 %collective-permute-start.84 = (bf16[512,1024]{1,0:T(8,128)(2,1)S(1)}, bf16[512,1024]{1,0:T(8,128)(2,1)S(1)}, u32[]{:S(2)}, u32[]{:S(2)}) collective-permute-start(bf16[512,1024]{1,0:T(8,128)(2,1)S(1)} %add_convert_fusion.5), channel_id=1, source_target_pairs={{0,4},{2,6},{4,0},{6,2},{8,12},{10,14},{12,8},{14,10},{16,20},{18,... | collective-permute-start | bytes 3145736 | tf_op jit(solution)/shard_map/ppermute | solution.py:76
  530.6 78.6 %collective-permute-start.76 = (bf16[512,1536]{1,0:T(8,128)(2,1)}, bf16[512,1536]{1,0:T(8,128)(2,1)}, u32[]{:S(2)}, u32[]{:S(2)}) collective-permute-start(bf16[512,1536]{1,0:T(8,128)(2,1)} %fusion.6), channel_id=1, source_target_pairs={{0,4},{2,6},{4,0},{6,2},{8,12},{10,14},{12,8},{14,10},{16,20},{18,... | collective-permute-start | bytes 4718600 | tf_op jit(solution)/shard_map/ppermute | solution.py:76
  556.0 86.0 %collective-permute-start.98 = (bf16[128,1024]{1,0:T(8,128)(2,1)}, bf16[128,1024]{1,0:T(8,128)(2,1)}, u32[]{:S(2)}, u32[]{:S(2)}) collective-permute-start(bf16[128,1024]{1,0:T(8,128)(2,1)} %get-tuple-element.129), channel_id=1, source_target_pairs={{0,24},{2,26},{4,28},{6,30},{8,16},{10,18},{12,20},{14,22},{16,8},... | collective-permute-start | bytes 786440 | tf_op jit(solution)/shard_map/ppermute | solution.py:82
  641.9 59.5 %collective-permute-start.91 = (bf16[128,2048]{1,0:T(8,128)(2,1)}, bf16[128,2048]{1,0:T(8,128)(2,1)S(1)}, u32[]{:S(2)}, u32[]{:S(2)}) collective-permute-start(bf16[128,2048]{1,0:T(8,128)(2,1)} %get-tuple-element.108), channel_id=1, source_target_pairs={{0,8},{2,10},{4,12},{6,14},{8,0},{10,2},{12,4},{14,6},{16,24},{18,... | collective-permute-start | bytes 1572872 | tf_op jit(solution)/shard_map/ppermute | solution.py:82
  642.0 60.8 %collective-permute-start.92 = (bf16[128,2048]{1,0:T(8,128)(2,1)}, bf16[128,2048]{1,0:T(8,128)(2,1)S(1)}, u32[]{:S(2)}, u32[]{:S(2)}) collective-permute-start(bf16[128,2048]{1,0:T(8,128)(2,1)} %get-tuple-element.106), channel_id=1, source_target_pairs={{0,16},{2,18},{4,20},{6,22},{8,24},{10,26},{12,28},{14,30},{16,0},... | collective-permute-start | bytes 1572872 | tf_op jit(solution)/shard_map/ppermute | solution.py:82
  646.3 64.4 %collective-permute-start.93 = (bf16[128,2048]{1,0:T(8,128)(2,1)}, bf16[128,2048]{1,0:T(8,128)(2,1)}, u32[]{:S(2)}, u32[]{:S(2)}) collective-permute-start(bf16[128,2048]{1,0:T(8,128)(2,1)} %get-tuple-element.105), channel_id=1, source_target_pairs={{0,24},{2,26},{4,28},{6,30},{8,16},{10,18},{12,20},{14,22},{16,8},... | collective-permute-start | bytes 1572872 | tf_op jit(solution)/shard_map/ppermute | solution.py:82
  649.3 73.3 %collective-permute-start.90 = (bf16[128,1024]{0,1:T(8,128)(2,1)}, bf16[128,1024]{0,1:T(8,128)(2,1)S(1)}, u32[]{:S(2)}, u32[]{:S(2)}) collective-permute-start(bf16[128,1024]{0,1:T(8,128)(2,1)} %add_convert_fusion.12), channel_id=1, source_target_pairs={{8,16},{10,18},{12,20},{14,22},{16,8},{18,10},{20,12},{22,14},{9,1... | collective-permute-start | bytes 786440 | tf_op jit(solution)/shard_map/ppermute | solution.py:82
  662.3 60.3 %collective-permute-start.88 = (bf16[128,1024]{0,1:T(8,128)(2,1)}, bf16[128,1024]{0,1:T(8,128)(2,1)}, u32[]{:S(2)}, u32[]{:S(2)}) collective-permute-start(bf16[128,1024]{0,1:T(8,128)(2,1)} %fusion.69), channel_id=1, source_target_pairs={{0,8},{2,10},{4,12},{6,14},{8,0},{10,2},{12,4},{14,6},{16,24},{18,... | collective-permute-start | bytes 786440 | tf_op jit(solution)/shard_map/ppermute | solution.py:82
  (177 other events, 4292.5 us)
